TPU v7x, 32 devices: a whole 2x2x4 slice. The times are simulated.
32 devices in a mesh: lat: 4 (over z), lon: 8 (over y, x, core).
Axes of the slice: x: 2, y: 2, z: 4, core: 2. Of those that a mesh axis runs over, the one named last changes fastest.
Arguments:
- latent: bfloat16 [48, 576, 512], P('lat', 'lon'), may hold values from -1000 to 1000
- w_qkv: bfloat16 [512, 1536], replicated, may hold values from -1 to 1
- w_proj: bfloat16 [512, 512], replicated, may hold values from -0.25 to 0.25
- w_fc1: bfloat16 [512, 2048], replicated, may hold values from -0.25 to 0.25
- w_fc2: bfloat16 [2048, 512], replicated, may hold values from -0.125 to 0.125
- w_head: bfloat16 [512, 1024], replicated, may hold values from -4 to 4
- target_bins: int32 [48, 576, 4], P('lat', 'lon'), may hold values from 0 to 255
- land_mask: int32 [48, 576], P('lat', 'lon'), may hold values 0 or 1
Outputs:
- grad_latent: bfloat16 [48, 576, 512], P('lat', 'lon')
- grad_qkv: float32 [512, 1536], P(('lat', 'lon'))
- grad_proj: float32 [512, 512], P(('lat', 'lon'))
- grad_fc1: float32 [512, 2048], P(('lat', 'lon'))
- grad_fc2: float32 [2048, 512], P(('lat', 'lon'))
- grad_head: float32 [512, 1024], P(('lat', 'lon'))
All inputs are finite; a program needn't handle non-finite values. No bound on the sum of `land_mask` on one device may be relied on, other than what follows from the above.
Results may differ from a plain program's by a relative error of at most 0.015.
Values may be sent and summed in bfloat16 or wider, within the bound.
A program may use at most 128 MiB of HBM per device.

v0:
```python
import math

import jax
import jax.numpy as jnp
from jax import lax
from jax.experimental import pallas as pl
from jax.experimental.pallas import tpu as pltpu
from jax.sharding import PartitionSpec as P

HEADS = 8
BINS = 256
VARS = 4
WIN_LAT = 6
WIN_LON = 12
HEAD_DIM = 64


eps = 1e-05
smear = 0.75
masked = -1e30


def shifted_2(value, axis, steps):
    count = lax.axis_size(axis)
    pairs = [(source, (source + steps) % count) for source in range(count)]
    return lax.ppermute(value, axis, pairs)


def normalize(values_in):
    centre = jnp.mean(values_in, -1, keepdims=True)
    offset = values_in - centre
    inverse = lax.rsqrt(jnp.mean(offset * offset, -1, keepdims=True) + eps)
    return (offset * inverse, inverse)


def norm_back(scaled, inverse, upstream):
    return inverse * (
        upstream
        - jnp.mean(upstream, -1, keepdims=True)
        - scaled * jnp.mean(upstream * scaled, -1, keepdims=True)
    )


def gelu_parts(pre_act):
    normal_cdf = 0.5 * (1.0 + jax.scipy.special.erf(pre_act / math.sqrt(2.0)))
    density = jnp.exp(-0.5 * pre_act * pre_act) / math.sqrt(2.0 * math.pi)
    return (pre_act * normal_cdf, normal_cdf + pre_act * density)


def dot_over(left, right, left_dim, right_dim):
    return lax.dot_general(
        left, right, (((left_dim,), (right_dim,)), ((), ())), preferred_element_type=jnp.float32
    )


def to_windows(block):
    row_count, col_count, feat_count = block.shape
    shaped = block.reshape(row_count // WIN_LAT, WIN_LAT, col_count // WIN_LON, WIN_LON, feat_count)
    return shaped.transpose(0, 2, 1, 3, 4).reshape(-1, feat_count)


def from_windows(packed, row_count, col_count):
    feat_count = packed.shape[-1]
    shaped = packed.reshape(
        row_count // WIN_LAT, col_count // WIN_LON, WIN_LAT, WIN_LON, feat_count
    )
    return shaped.transpose(0, 2, 1, 3, 4).reshape(row_count, col_count, feat_count)


def head_part(ref, part, head, width):
    start = part * width + head * HEAD_DIM
    return ref[0, :, start : start + HEAD_DIM]


def attention_kernel(qkv_ref, allowed_ref, context_ref, probs_ref):
    width = context_ref.shape[-1]
    allowed = allowed_ref[0] > 0.5
    pieces = []
    for head in range(HEADS):
        query = head_part(qkv_ref, 0, head, width)
        key = head_part(qkv_ref, 1, head, width)
        value = head_part(qkv_ref, 2, head, width)
        scores = dot_over(query, key, 1, 1) * HEAD_DIM ** (-0.5)
        scores = jnp.where(allowed, scores, masked)
        exponent = jnp.exp(scores - jnp.max(scores, -1, keepdims=True))
        probs = exponent / jnp.sum(exponent, -1, keepdims=True)
        probs_ref[0, head] = probs
        pieces.append(dot_over(probs.astype(jnp.bfloat16), value, 1, 0))
    context_ref[0] = jnp.concatenate(pieces, -1).astype(jnp.bfloat16)


def attention_back_kernel(qkv_ref, probs_ref, d_context_ref, d_qkv_ref):
    width = d_context_ref.shape[-1]
    d_queries, d_keys, d_values = [], [], []
    for head in range(HEADS):
        query = head_part(qkv_ref, 0, head, width)
        key = head_part(qkv_ref, 1, head, width)
        value = head_part(qkv_ref, 2, head, width)
        upstream = head_part(d_context_ref, 0, head, width)
        probs = probs_ref[0, head]
        d_probs = dot_over(upstream, value, 1, 1)
        d_scores = (
            probs
            * (d_probs - jnp.sum(d_probs * probs, -1, keepdims=True))
            * HEAD_DIM ** (-0.5)
        )
        d_scores_t = d_scores.T.astype(jnp.bfloat16)
        d_scores = d_scores.astype(jnp.bfloat16)
        d_queries.append(dot_over(d_scores, key, 1, 0))
        d_keys.append(dot_over(d_scores_t, query, 1, 0))
        d_values.append(dot_over(probs.T.astype(jnp.bfloat16), upstream, 1, 0))
    for part, pieces in enumerate((d_queries, d_keys, d_values)):
        joined = jnp.concatenate(pieces, -1).astype(jnp.bfloat16)
        d_qkv_ref[0, :, part * width : (part + 1) * width] = joined


def whole_block(*dims):
    return pl.BlockSpec((1, *dims), lambda place: (place,) + (0,) * len(dims))


def attention(qkv_all, allowed, windows_across):
    windows, tokens, triple = qkv_all.shape
    width = triple // 3
    return pl.pallas_call(
        attention_kernel,
        grid=(windows,),
        in_specs=[
            whole_block(tokens, triple),
            pl.BlockSpec((1, tokens, tokens), lambda place: (place // windows_across, 0, 0)),
        ],
        out_specs=[whole_block(tokens, width), whole_block(HEADS, tokens, tokens)],
        out_shape=[
            jax.ShapeDtypeStruct((windows, tokens, width), jnp.bfloat16),
            jax.ShapeDtypeStruct((windows, HEADS, tokens, tokens), jnp.float32),
        ],
        cost_estimate=pl.CostEstimate(
            flops=4 * windows * tokens * tokens * width * 20, bytes_accessed=8000000, transcendentals=0
        ),
        name="attention",
    )(qkv_all, allowed)


def attention_back(qkv_all, probs, d_context):
    windows, tokens, triple = qkv_all.shape
    width = triple // 3
    return pl.pallas_call(
        attention_back_kernel,
        grid=(windows,),
        in_specs=[
            whole_block(tokens, triple),
            whole_block(HEADS, tokens, tokens),
            whole_block(tokens, width),
        ],
        out_specs=whole_block(tokens, triple),
        out_shape=jax.ShapeDtypeStruct((windows, tokens, triple), jnp.bfloat16),
        cost_estimate=pl.CostEstimate(
            flops=8 * windows * tokens * tokens * width * 20, bytes_accessed=10000000, transcendentals=0
        ),
        name="attention_back",
    )(qkv_all, probs, d_context)


def target_table():
    edges = jnp.arange(BINS + 1, dtype=jnp.int32).astype(jnp.float32)
    centre = jnp.arange(BINS, dtype=jnp.int32).astype(jnp.float32)[:, None] + 0.5
    cumulative = 0.5 * jax.scipy.special.erf((edges - centre) / (smear * math.sqrt(2.0)))
    table = (cumulative[:, 1:] - cumulative[:, :-1]) / (cumulative[:, -1:] - cumulative[:, :1])
    upper = lax.reduce_precision(table, 8, 7)
    lower = (table - upper).astype(jnp.bfloat16)
    return (upper.astype(jnp.bfloat16), lower)


def head_grad(normed3, w_head, target_bins, land_mask):
    upper, lower = target_table()
    weight_tok = land_mask.astype(jnp.float32) / VARS
    bins = jnp.arange(BINS, dtype=jnp.int32)[None, :]
    pieces = []
    for var in range(VARS):
        logits = jnp.dot(
            normed3,
            w_head[:, var * BINS : (var + 1) * BINS],
            preferred_element_type=jnp.float32,
        )
        exponent = jnp.exp(logits - jnp.max(logits, -1, keepdims=True))
        bin_probs = exponent / jnp.sum(exponent, -1, keepdims=True)
        picked = (target_bins[:, var : var + 1] == bins).astype(jnp.bfloat16)
        target = jnp.dot(picked, upper, preferred_element_type=jnp.float32) + jnp.dot(
            picked, lower, preferred_element_type=jnp.float32
        )
        pieces.append((weight_tok * (bin_probs - target)).astype(jnp.bfloat16))
    return jnp.concatenate(pieces, 1)


def roll_ahead(block):
    half_rows = WIN_LAT // 2
    half_cols = WIN_LON // 2
    edge_cols = shifted_2(block[:, :half_cols], "lon", -1)
    moved_cols = jnp.concatenate([block[:, half_cols:], edge_cols], 1)
    edge_rows = shifted_2(moved_cols[:half_rows], "lat", -1)
    return jnp.concatenate([moved_cols[half_rows:], edge_rows], 0)


def roll_behind(block):
    half_rows = WIN_LAT // 2
    half_cols = WIN_LON // 2
    row_count, col_count = (block.shape[0], block.shape[1])
    edge_cols = shifted_2(block[:, col_count - half_cols :], "lon", 1)
    moved_cols = jnp.concatenate([edge_cols, block[:, : col_count - half_cols]], 1)
    edge_rows = shifted_2(moved_cols[row_count - half_rows :], "lat", 1)
    return jnp.concatenate([edge_rows, moved_cols[: row_count - half_rows]], 0)


def scatter_over(value, axis):
    return lax.psum_scatter(value, axis, scatter_dimension=0, tiled=True)


def local(latent, w_qkv, w_proj, w_fc1, w_fc2, w_head, target_bins, land_mask):
    row_count, col_count, feat_width = latent.shape
    half_rows = WIN_LAT // 2
    tokens = WIN_LAT * WIN_LON
    lat_total = row_count * lax.axis_size("lat")
    devices = lax.axis_size("lat") * lax.axis_size("lon")
    row_place = (
        lax.axis_index("lat") * row_count + jnp.arange(row_count, dtype=jnp.int32) + half_rows
    )
    row_labels = (row_place >= lat_total).astype(jnp.int32)
    window_tags = jnp.repeat(row_labels.reshape(-1, WIN_LAT), WIN_LON, axis=1)
    allowed = (window_tags[:, :, None] == window_tags[:, None, :]).astype(jnp.float32)
    marks = jnp.concatenate([target_bins, land_mask[:, :, None]], 2)
    residual_in = to_windows(roll_ahead(latent)).astype(jnp.float32)
    marks = to_windows(roll_ahead(marks))
    scaled1, inverse1 = normalize(residual_in)
    shifted = scaled1.astype(jnp.bfloat16)
    qkv_all = jnp.dot(shifted, w_qkv, preferred_element_type=jnp.float32).astype(jnp.bfloat16)
    qkv_all = qkv_all.reshape(-1, tokens, 3 * feat_width)
    context, attn_probs = attention(qkv_all, allowed, col_count // WIN_LON)
    context = context.reshape(-1, feat_width)
    attended = jnp.dot(context, w_proj, preferred_element_type=jnp.float32).astype(jnp.bfloat16)
    residual = residual_in + attended.astype(jnp.float32)
    scaled2, inverse2 = normalize(residual)
    normed2 = scaled2.astype(jnp.bfloat16)
    pre_act = jnp.dot(normed2, w_fc1, preferred_element_type=jnp.float32)
    activated, gelu_slope = gelu_parts(pre_act)
    activated = activated.astype(jnp.bfloat16)
    block_out = residual + jnp.dot(activated, w_fc2, preferred_element_type=jnp.float32)
    scaled3, inverse3 = normalize(block_out)
    normed3 = scaled3.astype(jnp.bfloat16)
    d_logits = head_grad(normed3, w_head, marks[:, :VARS], marks[:, VARS:])
    grad_head = jnp.dot(normed3.T, d_logits, preferred_element_type=jnp.float32)
    d_out = norm_back(
        scaled3, inverse3, jnp.dot(d_logits, w_head.T, preferred_element_type=jnp.float32)
    )
    d_outb = d_out.astype(jnp.bfloat16)
    grad_fc2 = jnp.dot(activated.T, d_outb, preferred_element_type=jnp.float32)
    d_pre = (jnp.dot(d_outb, w_fc2.T, preferred_element_type=jnp.float32) * gelu_slope).astype(
        jnp.bfloat16
    )
    grad_fc1 = jnp.dot(normed2.T, d_pre, preferred_element_type=jnp.float32)
    d_resid = d_out + norm_back(
        scaled2, inverse2, jnp.dot(d_pre, w_fc1.T, preferred_element_type=jnp.float32)
    )
    d_attended = d_resid.astype(jnp.bfloat16)
    grad_proj = jnp.dot(context.T, d_attended, preferred_element_type=jnp.float32)
    grads = [grad.astype(jnp.bfloat16) for grad in (grad_head, grad_fc1, grad_proj)]
    ratio = grad_fc2.shape[0] // feat_width
    low_fc2 = grad_fc2.astype(jnp.bfloat16).reshape(
        devices, ratio, feat_width // devices, feat_width
    )
    grads += [low_fc2[:, part].reshape(feat_width, feat_width) for part in range(ratio)]
    joined, d_attended = lax.optimization_barrier((jnp.concatenate(grads, 1), d_attended))
    early = scatter_over(joined, "lat")
    d_context = jnp.dot(d_attended, w_proj.T, preferred_element_type=jnp.float32).astype(
        jnp.bfloat16
    )
    d_qkv = attention_back(
        qkv_all, attn_probs, d_context.reshape(-1, tokens, feat_width)
    ).reshape(-1, 3 * feat_width)
    grad_qkv = jnp.dot(shifted.T, d_qkv, preferred_element_type=jnp.float32)
    late = scatter_over(grad_qkv.astype(jnp.bfloat16), "lat")
    summed = scatter_over(jnp.concatenate([late, early], 1), "lon").astype(jnp.float32)
    late, early = summed[:, : 3 * feat_width], summed[:, 3 * feat_width :]
    d_shifted = jnp.dot(d_qkv, w_qkv.T, preferred_element_type=jnp.float32).astype(jnp.bfloat16)
    grad_latent = (d_resid + norm_back(scaled1, inverse1, d_shifted.astype(jnp.float32))).astype(
        jnp.bfloat16
    )
    grad_latent = roll_behind(from_windows(grad_latent, row_count, col_count))
    cuts = [grad_head.shape[1], grad_fc1.shape[1], grad_proj.shape[1]]
    first, second, third = cuts[0], cuts[0] + cuts[1], sum(cuts)
    sum_fc2 = early[:, third:].reshape(-1, ratio, feat_width).transpose(1, 0, 2)
    return (
        grad_latent,
        late,
        early[:, second:third],
        early[:, first:second],
        sum_fc2.reshape(-1, feat_width),
        early[:, :first],
    )


def solution(mesh):
    placed = (
        P("lat", "lon", None),
        P(),
        P(),
        P(),
        P(),
        P(),
        P("lat", "lon", None),
        P("lat", "lon"),
    )
    return jax.shard_map(
        local,
        mesh=mesh,
        in_specs=placed,
        out_specs=(
            P("lat", "lon", None),
            P(("lat", "lon"), None),
            P(("lat", "lon"), None),
            P(("lat", "lon"), None),
            P(("lat", "lon"), None),
            P(("lat", "lon"), None),
        ),
        check_vma=False,
    )
```

profile of v0, /device:TPU:0, one launch (start us, length us, event | category | flops | bytes accessed | tf_op | source)
XLA Modules:
  0.0 360.5 jit_solution(6954859639485760151)
XLA Ops:
  8.8 3.4 collective-permute-start.2
  12.2 1.5 slice.169
  17.4 3.6 collective-permute-start.3
  21.0 1.3 collective-permute-done.3
  25.6 1.3 fusion.32
  26.9 1.3 fusion.33
  28.3 1.2 fusion.34
  29.5 4.1 %collective-permute-start.1 = (bf16[3,72,512]{2,1,0:T(8,128)(2,1)S(1)}, bf16[3,72,512]{2,1,0:T(8,128)(2,1)S(1)}, u32[]{:S(2)}, u32[]{:S(2)}) collective-permute-start(bf16[3,72,512]{2,1,0:T(8,128)(2,1)S(1)} %pad_maximum_fusion.6), channel_id=1, source_target_pairs={{0,24},{8,0},{16,8},{24,16},{1,25},{9,1},{17,9},{25,17},{2,26},{10... | collective-permute-start | bytes 663560 | tf_op jit(solution)/shard_map/ppermute | solution.py:26
  33.8 3.4 collective-permute-done.1
  37.2 1.3 maximum_convert_fusion
  38.5 2.7 reshape.179
  41.2 2.0 bitcast_reduce_fusion
  44.7 3.4 copy.37
  48.2 2.6 reshape.177
  50.8 5.1 %convolution_convert_fusion = bf16[864,1536]{1,0:T(8,128)(2,1)} fusion(bf16[512,1536]{1,0:T(8,128)(2,1)} %param.9, f32[864,512]{1,0:T(8,128)} %reshape.177, f32[864]{0:T(1024)S(1)} %rsqrt.29, f32[864]{0:T(1024)S(1)} %div.161), kind=kOutput, calls=%fused_computation.9 | convolution fusion | flops 1361608704 | bytes 6003456 | tf_op jit(solution)/shard_map/dot_general | solution.py:234
  55.9 14.1 %attention.1 = (bf16[12,72,512]{2,1,0:T(8,128)(2,1)}, f32[12,8,72,72]{3,2,1,0:T(8,128)}) custom-call(bf16[12,72,1536]{2,1,0:T(8,128)(2,1)} %bitcast.81, f32[2,72,72]{2,1,0:T(8,128)} %compare_convert_fusion.allowed_ref), custom_call_target="tpu_custom_call" | custom-call | flops 2548039680 | bytes 8000000 | tf_op jit(solution)/shard_map/attention/pallas_call | solution.py:124
  69.9 2.6 fusion.76
  73.0 5.0 %multiply_convert_fusion = (bf16[864,2048]{1,0:T(8,128)(2,1)S(1)}, f32[864,2048]{1,0:T(8,128)}) fusion(bf16[512,2048]{1,0:T(8,128)(2,1)S(1)} %copy-done, f32[864,512]{1,0:T(8,128)S(1)} %get-tuple-element.35, f32[864]{0:T(1024)S(1)} %add_rsqrt_fusion.2, f32[864]{0:T(1024)S(1)} %broadcast_multiply_fusion.8), kind=kOutput, calls=%fused_computation.7 | convolution fusion | flops 1822113792 | bytes 14490368 | tf_op jit(solution)/shard_map/dot_general | solution.py:242
  78.1 2.1 fusion.77
  89.7 2.4 fusion.72
  92.1 2.3 fusion.12
  95.5 1.4 convert_element_type.205
  96.9 2.7 subtract_multiply_fusion
  99.6 4.6 %convolution_convert_fusion.2 = bf16[2048,512]{1,0:T(8,128)(2,1)S(1)} fusion(bf16[864,2048]{1,0:T(8,128)(2,1)} %copy-done.19, f32[864,512]{1,0:T(8,128)S(1)} %subtract_multiply_fusion), kind=kOutput, calls=%fused_computation.11 | convolution fusion | flops 1813430272 | bytes 7405568 | tf_op jit(solution)/shard_map/dot_general | solution.py:254
  104.2 4.3 %fusion.5 = bf16[864,2048]{1,0:T(8,128)(2,1)S(1)} fusion(f32[864,2048]{1,0:T(8,128)S(1)} %bitcast.87, bf16[2048,512]{1,0:T(8,128)(2,1)S(1)} %copy-done.18, f32[864,512]{1,0:T(8,128)S(1)} %subtract_multiply_fusion), kind=kOutput, calls=%fused_computation.6 | convolution fusion | flops 1830076416 | bytes 14483456 | tf_op jit(solution)/shard_map/dot_general | solution.py:255
  108.7 1.3 copy-done.3
  110.0 2.2 fusion.71
  112.2 4.0 %fusion.6 = bf16[512,5632]{1,0:T(8,128)(2,1)} fusion(bf16[512,5632]{1,0:T(8,128)(2,1)} %fusion.12, bf16[864,2048]{1,0:T(8,128)(2,1)S(1)} %fusion.5, f32[864,512]{1,0:T(8,128)S(1)} %copy-done.3, f32[864]{0:T(1024)S(1)} %add_rsqrt_fusion.2, f32[864]{0:T(1024)S(1)} %broadcast_multiply_fusion.8), kind=kOutput, calls=%fused_computation.13 | convolution fusion | flops 1814315008 | bytes 7412480 | tf_op jit(solution)/shard_map/dot_general | solution.py:258
  116.1 1.8 fusion.73
  117.9 1.6 fusion.24
  123.1 2.7 convolution_convert_fusion.6
  125.9 34.3 %attention_back.1 = bf16[12,72,1536]{2,1,0:T(8,128)(2,1)} custom-call(bf16[12,72,1536]{2,1,0:T(8,128)(2,1)} %bitcast.82, f32[12,8,72,72]{3,2,1,0:T(8,128)} %get-tuple-element.11.probs_ref, bf16[12,72,512]{2,1,0:T(8,128)(2,1)} %bitcast.85), custom_call_target="tpu_custom_call" | custom-call | flops 5096079360 | bytes 10000000 | tf_op jit(solution)/shard_map/attention_back/pallas_call | solution.py:146
  160.2 4.7 %convolution_convert_fusion.1 = bf16[512,1536]{1,0:T(8,128)(2,1)} fusion(bf16[864,512]{1,0:T(8,128)(2,1)S(1)} %convert_element_type.205, bf16[864,1536]{1,0:T(8,128)(2,1)} %bitcast.83), kind=kOutput, calls=%fused_computation.10 | convolution fusion | flops 1359740928 | bytes 5111808 | tf_op jit(solution)/shard_map/dot_general | solution.py:278
  165.7 34.8 %reduce-scatter.4.cloned.1.call-done = bf16[128,1536]{1,0:T(8,128)(2,1)} async-done(((bf16[512,1536]{1,0:T(8,128)(2,1)}), bf16[128,1536]{1,0:T(8,128)(2,1)}) %reduce-scatter.4.cloned.1.call-update) | async-done | bytes 393232 | tf_op jit(solution)/shard_map/reduce_scatter | solution.py:214
  200.6 103.5 %reduce-scatter.6.cloned.1.call-done = bf16[128,5632]{1,0:T(8,128)(2,1)} async-done(((bf16[512,5632]{1,0:T(8,128)(2,1)}), bf16[128,5632]{1,0:T(8,128)(2,1)}) %reduce-scatter.6.cloned.1.call-update) | async-done | bytes 1441808 | tf_op jit(solution)/shard_map/reduce_scatter | solution.py:214
  304.0 2.8 pad_maximum_fusion
  306.9 4.6 %convert_reduce_fusion = (f32[864]{0:T(1024)S(1)}, f32[864]{0:T(1024)S(1)}, bf16[864,512]{1,0:T(8,128)(2,1)S(1)}) fusion(f32[864]{0:T(1024)S(1)} %rsqrt.29, f32[864,512]{1,0:T(8,128)} %reshape.177, f32[864]{0:T(1024)S(1)} %div.161, bf16[864,1536]{1,0:T(8,128)(2,1)} %bitcast.84, bf16[512,1536]{1,0:T(8,128)(2,1)} %param.9), kind=kOutput, calls=%fused_computation.16 | convolution fusion | flops 1362049280 | bytes 6895104 | tf_op jit(solution)/shard_map/dot_general | solution.py:282
  311.5 1.6 fusion.10
  313.1 1.3 reshape.173
  315.5 1.4 reshape.174
  317.0 4.9 %collective-permute-done.4 = bf16[12,6,512]{2,1,0:T(8,128)(2,1)S(1)} collective-permute-done((bf16[12,6,512]{2,1,0:T(8,128)(2,1)S(1)}, bf16[12,6,512]{2,1,0:T(8,128)(2,1)S(1)}, u32[]{:S(2)}, u32[]{:S(2)}) %collective-permute-start.4) | collective-permute-done | bytes 73760 | tf_op jit(solution)/shard_map/ppermute | solution.py:26
  322.0 1.6 collective-permute-start.5
  323.6 6.2 %collective-permute-done.5 = bf16[3,72,512]{2,1,0:T(8,128)(2,1)S(1)} collective-permute-done((bf16[3,72,512]{2,1,0:T(8,128)(2,1)S(1)}, bf16[3,72,512]{2,1,0:T(8,128)(2,1)S(1)}, u32[]{:S(2)}, u32[]{:S(2)}) %collective-permute-start.5) | collective-permute-done | bytes 221216 | tf_op jit(solution)/shard_map/ppermute | solution.py:26
  330.9 16.6 %reduce-scatter.8.cloned.1.call-done = bf16[16,7168]{1,0:T(8,128)(2,1)} async-done(((bf16[128,7168]{1,0:T(8,128)(2,1)}), bf16[16,7168]{1,0:T(8,128)(2,1)}) %reduce-scatter.8.cloned.1.call-update) | async-done | bytes 229392 | tf_op jit(solution)/shard_map/reduce_scatter | solution.py:214
  347.5 1.5 fusion.75
  349.8 1.3 slice.224
  351.2 1.4 slice.227
  352.6 1.4 slice.223
  (123 shorter events, 28.8 us)
Async XLA Ops:
  7.2 65.8 %copy-start = (bf16[512,2048]{1,0:T(8,128)(2,1)S(1)}, bf16[512,2048]{1,0:T(8,128)(2,1)}, u32[]{:S(2)}) copy-start(bf16[512,2048]{1,0:T(8,128)(2,1)} %param.11) | copy-start | bytes 6291460
  7.2 193.4 %reduce-scatter.4.cloned.1.call-start = ((), (), s32[]{:S(2)}) async-start(), calls=%async_computation.3 | async-start | bytes 1966080 | tf_op jit(solution)/shard_map/reduce_scatter | solution.py:214
  8.8 8.4 %collective-permute-start.2 = (s32[12,6,5]{1,2,0:T(8,128)S(1)}, s32[12,6,5]{1,2,0:T(8,128)S(1)}, u32[]{:S(2)}, u32[]{:S(2)}) collective-permute-start(s32[12,6,5]{1,2,0:T(8,128)S(1)} %pad_add_fusion), channel_id=1, source_target_pairs={{0,7},{1,0},{2,1},{3,2},{4,3},{5,4},{6,5},{7,6},{8,15},{9,8},{10,9... | collective-permute-start | bytes 4328 | tf_op jit(solution)/shard_map/ppermute | solution.py:26
  13.8 15.7 %collective-permute-start = (bf16[12,6,512]{2,1,0:T(8,128)(2,1)}, bf16[12,6,512]{2,1,0:T(8,128)(2,1)S(1)}, u32[]{:S(2)}, u32[]{:S(2)}) collective-permute-start(bf16[12,6,512]{2,1,0:T(8,128)(2,1)} %slice.169), channel_id=1, source_target_pairs={{0,7},{1,0},{2,1},{3,2},{4,3},{5,4},{6,5},{7,6},{8,15},{9,8},{10,9... | collective-permute-start | bytes 221192 | tf_op jit(solution)/shard_map/ppermute | solution.py:26
  14.6 2.4 copy-start.7
  17.4 5.0 %collective-permute-start.3 = (s32[3,72,5]{1,2,0:T(8,128)S(1)}, s32[3,72,5]{1,2,0:T(8,128)S(1)}, u32[]{:S(2)}, u32[]{:S(2)}) collective-permute-start(s32[3,72,5]{1,2,0:T(8,128)S(1)} %pad_add_fusion.2), channel_id=1, source_target_pairs={{0,24},{8,0},{16,8},{24,16},{1,25},{9,1},{17,9},{25,17},{2,26},{10... | collective-permute-start | bytes 12968 | tf_op jit(solution)/shard_map/ppermute | solution.py:26
  29.5 7.7 %collective-permute-start.1 = (bf16[3,72,512]{2,1,0:T(8,128)(2,1)S(1)}, bf16[3,72,512]{2,1,0:T(8,128)(2,1)S(1)}, u32[]{:S(2)}, u32[]{:S(2)}) collective-permute-start(bf16[3,72,512]{2,1,0:T(8,128)(2,1)S(1)} %pad_maximum_fusion.6), channel_id=1, source_target_pairs={{0,24},{8,0},{16,8},{24,16},{1,25},{9,1},{17,9},{25,17},{2,26},{10... | collective-permute-start | bytes 663560 | tf_op jit(solution)/shard_map/ppermute | solution.py:26
  41.2 2.4 copy-start.1
  72.6 5.5 %copy-start.2 = (f32[864,512]{1,0:T(8,128)}, f32[864,512]{1,0:T(8,128)S(1)}, u32[]{:S(2)}) copy-start(f32[864,512]{1,0:T(8,128)S(1)} %get-tuple-element.35) | copy-start | bytes 5308420
  73.0 5.0 %copy-start.17 = (bf16[2048,512]{1,0:T(8,128)(2,1)S(1)}, bf16[2048,512]{1,0:T(8,128)(2,1)}, u32[]{:S(2)}) copy-start(bf16[2048,512]{1,0:T(8,128)(2,1)} %param.12) | copy-start | bytes 6291460
  78.1 2.1 copy-start.19
  80.1 9.6 %copy-start.5 = (f32[864,512]{1,0:T(8,128)}, f32[864,512]{1,0:T(8,128)S(1)}, u32[]{:S(2)}) copy-start(f32[864,512]{1,0:T(8,128)S(1)} %get-tuple-element.39) | copy-start | bytes 5308420
  80.6 1.4 copy-start.8
  83.4 1.2 copy-start.12
  83.4 1.2 copy-start.16
  84.6 1.2 copy-start.11
  85.8 1.3 copy-start.10
  87.1 1.4 copy-start.9
  96.9 7.3 %slice-start = ((s8[7077888]{0:T(1024)(128)(4,1)}), s8[4194304]{0:T(1024)(128)(4,1)S(1)}, s32[]{:S(2)}) async-start(s8[7077888]{0:T(1024)(128)(4,1)} %bitcast.86), calls=%async_computation.6 | async-start | bytes 8388608
  99.6 4.6 %copy-start.18 = (bf16[2048,512]{1,0:T(8,128)(2,1)S(1)}, bf16[2048,512]{1,0:T(8,128)(2,1)}, u32[]{:S(2)}) copy-start(bf16[2048,512]{1,0:T(8,128)(2,1)} %param.12) | copy-start | bytes 6291460
  99.6 4.6 %slice-start.1 = ((s8[7077888]{0:T(1024)(128)(4,1)}), s8[2883584]{0:T(1024)(128)(4,1)S(1)}, s32[]{:S(2)}) async-start(s8[7077888]{0:T(1024)(128)(4,1)} %bitcast.86), calls=%async_computation.7 | async-start | bytes 5767168
  108.5 1.5 copy-start.3
  116.1 1.8 copy-start.13
  117.9 2.6 copy-start.14
  120.5 2.7 copy-start.15
  164.9 139.1 %reduce-scatter.6.cloned.1.call-start = ((), (), s32[]{:S(2)}) async-start(), calls=%async_computation.4 | async-start | bytes 7208960 | tf_op jit(solution)/shard_map/reduce_scatter | solution.py:214
  165.7 181.8 %reduce-scatter.8.cloned.1.call-start = ((), (), s32[]{:S(2)}) async-start(), calls=%async_computation.5 | async-start | bytes 2064384 | tf_op jit(solution)/shard_map/reduce_scatter | solution.py:214
  306.9 4.6 %copy-start.4 = (f32[864,512]{1,0:T(8,128)S(1)}, f32[864,512]{1,0:T(8,128)}, u32[]{:S(2)}) copy-start(f32[864,512]{1,0:T(8,128)} %reshape.177) | copy-start | bytes 5308420
  306.9 4.6 %copy-start.6 = (f32[864,512]{1,0:T(8,128)S(1)}, f32[864,512]{1,0:T(8,128)}, u32[]{:S(2)}) copy-start(f32[864,512]{1,0:T(8,128)} %get-tuple-element.25) | copy-start | bytes 5308420
  317.0 5.0 %collective-permute-start.4 = (bf16[12,6,512]{2,1,0:T(8,128)(2,1)S(1)}, bf16[12,6,512]{2,1,0:T(8,128)(2,1)S(1)}, u32[]{:S(2)}, u32[]{:S(2)}) collective-permute-start(bf16[12,6,512]{2,1,0:T(8,128)(2,1)S(1)} %slice.221), channel_id=1, source_target_pairs={{0,1},{1,2},{2,3},{3,4},{4,5},{5,6},{6,7},{7,0},{8,9},{9,10},{10,1... | collective-permute-start | bytes 221192 | tf_op jit(solution)/shard_map/ppermute | solution.py:26
  322.0 7.8 %collective-permute-start.5 = (bf16[3,72,512]{2,1,0:T(8,128)(2,1)S(1)}, bf16[3,72,512]{2,1,0:T(8,128)(2,1)S(1)}, u32[]{:S(2)}, u32[]{:S(2)}) collective-permute-start(bf16[3,72,512]{2,1,0:T(8,128)(2,1)S(1)} %pad_maximum_fusion.5), channel_id=1, source_target_pairs={{0,8},{8,16},{16,24},{24,0},{1,9},{9,17},{17,25},{25,1},{2,10},{10... | collective-permute-start | bytes 663560 | tf_op jit(solution)/shard_map/ppermute | solution.py:26
Sparse Core Ops, SparseCore 0:
  165.0 35.4 reduce-scatter.3
  202.9 101.1 reduce-scatter.5
  307.4 40.0 reduce-scatter.7
where the time goes:
time: 362 us; the launch traced here: 361 us
  waiting for transfers between devices  172 us (48%)
  matrix products  59.3 us (16%)
  Pallas kernels  48.4 us (13%)
  local copies, waits for them, and re-layouts  33.3 us (9%)
  other arithmetic  20.1 us (6%)
  between operations  14.3 us (4%)
  starting transfers between devices  13.6 us (4%)
    reduce_scatter x3, waiting for transfers between devices, scatter_over(): return lax.psum_scatter(value, axis, scatter_dimension=0, tiled=True)  155 us
    pallas_call x1, Pallas kernels, attention_back(): pl.pallas_call(attention_back_kernel, grid=(windows,), in_specs=[whole_bl...  34.3 us
    ppermute x6, waiting for transfers between devices, shifted_2(): return lax.ppermute(value, axis, pairs)  15.9 us
    pallas_call x1, Pallas kernels, attention(): pl.pallas_call(attention_kernel, grid=(windows,), in_specs=[whole_block(t...  14.1 us
    ppermute x6, starting transfers between devices, shifted_2(): return lax.ppermute(value, axis, pairs)  13.4 us
    convert_element_type x3, local copies, waits for them, and re-layouts, local(): residual_in = to_windows(roll_ahead(latent)).astype(jnp.float32)  8.76 us
  transfers between devices with their start and end apart: 9, of which 7 were waited for; matrix products, arithmetic and copies ran while one was open for 6% of the time, Pallas kernels for 0%

commit v1 on v0

v1 whole, which is shorter than its diff:
```python
import functools
import math
import types

import jax
import jax.numpy as jnp
from jax import lax
from jax.experimental import pallas as pl
from jax.experimental.pallas import tpu as pltpu
from jax.sharding import PartitionSpec as P

HEADS = 8
BINS = 256
VARS = 4
WIN_LAT = 6
WIN_LON = 12
HEAD_DIM = 64
TOKENS = WIN_LAT * WIN_LON
HALF_ROWS = WIN_LAT // 2
HALF_COLS = WIN_LON // 2
EDGE = 8
LANES = 128
TILE = 256

eps = 1e-05
smear = 0.75
masked = -1e30
SOFTMAX_SCALE = HEAD_DIM ** (-0.5) / math.log(2.0)
GROUP = 2
F32 = jnp.float32
BF16 = jnp.bfloat16


def dot_nn(left, right):
    return lax.dot_general(left, right, (((1,), (0,)), ((), ())), preferred_element_type=F32)


def dot_nt(left, right):
    return lax.dot_general(left, right, (((1,), (1,)), ((), ())), preferred_element_type=F32)


def normalize(values_in):
    centre = jnp.mean(values_in, -1, keepdims=True)
    offset = values_in - centre
    inverse = lax.rsqrt(jnp.mean(offset * offset, -1, keepdims=True) + eps)
    return (offset * inverse, inverse)


def norm_back(scaled, inverse, upstream):
    return inverse * (
        upstream
        - jnp.mean(upstream, -1, keepdims=True)
        - scaled * jnp.mean(upstream * scaled, -1, keepdims=True)
    )


def loop(count, body):
    def step(place, carry):
        body(place)
        return carry

    lax.fori_loop(0, count, step, 0)


def rows_at(place, size):
    return pl.ds(pl.multiple_of(place * size, math.gcd(size, 16)), size)


def cols_at(place, size=TILE):
    return pl.ds(pl.multiple_of(place * size, size), size)


def row_block(count, most):
    best = 16
    for size in range(16, most + 1, 16):
        if count % size == 0:
            best = size
    return best


def pair_stack(block):
    lane = lax.broadcasted_iota(jnp.int32, block.shape, 1)
    low = lane < HEAD_DIM
    return jnp.concatenate([jnp.where(low, block, 0.0), jnp.where(low, 0.0, block)], 0).astype(BF16)


def pair_merge(stacked):
    top, bottom = stacked[:TOKENS], stacked[TOKENS:]
    lane = lax.broadcasted_iota(jnp.int32, top.shape, 1)
    return jnp.where(lane < HEAD_DIM, top, bottom)


def cut_windows(main, east, south, corner, strip, wins):
    row_count, col_count = main.shape[0], main.shape[1]
    own_rows = row_count - HALF_ROWS
    across, pitch = col_count // WIN_LON, col_count + EDGE
    for row in range(row_count):
        if row < own_rows:
            body, edge = main[row + HALF_ROWS], east[row + HALF_ROWS]
        else:
            body, edge = south[row - own_rows], corner[row - own_rows]
        strip[row * pitch : row * pitch + col_count] = body.astype(F32)
        strip[row * pitch + col_count : (row + 1) * pitch] = edge.astype(F32)[:EDGE]
    for row in range(row_count):
        for col in range(across):
            start = ((row // WIN_LAT) * across + col) * TOKENS + (row % WIN_LAT) * WIN_LON
            first = row * pitch + HALF_COLS + col * WIN_LON
            wins[start : start + WIN_LON] = strip[first : first + WIN_LON]


def join_windows(wins, strip, row_count, col_count):
    across, pitch = col_count // WIN_LON, col_count + EDGE
    for row in range(row_count):
        for col in range(across):
            start = ((row // WIN_LAT) * across + col) * TOKENS + (row % WIN_LAT) * WIN_LON
            first = row * pitch + HALF_COLS + col * WIN_LON
            strip[first : first + WIN_LON] = wins[start : start + WIN_LON]


def fill_table(upper, lower):
    scale = smear * math.sqrt(2.0)

    def mass_below(edge, centre):
        return 0.5 * lax.erf((edge - centre) / scale)

    def part(place):
        base = place * 64
        centre = (base + lax.broadcasted_iota(jnp.int32, (64, BINS), 0)).astype(F32) + 0.5
        edge = lax.broadcasted_iota(jnp.int32, (64, BINS), 1).astype(F32)
        whole = mass_below(float(BINS), centre) - mass_below(0.0, centre)
        table = (mass_below(edge + 1.0, centre) - mass_below(edge, centre)) / whole
        high = table.astype(BF16)
        upper[pl.ds(pl.multiple_of(base, 64), 64)] = high
        lower[pl.ds(pl.multiple_of(base, 64), 64)] = (table - high.astype(F32)).astype(BF16)

    loop(BINS // 64, part)


class Summed:
    def __init__(self, link, refs, out):
        self.link, self.out = link, out
        self.whole, self.pair, self.first, self.second, self.plane, self.slots = refs[:6]
        self.semaphores = refs[6:]
        self.half = self.plane.shape[-1] // 2
        self.copies = []

    def copy(self, place, source, target, where):
        send, recv = self.semaphores
        made = pltpu.make_async_remote_copy(
            src_ref=source, dst_ref=target, send_sem=send.at[place], recv_sem=recv.at[place],
            device_id=where, device_id_type=pl.DeviceIdType.MESH,
        )
        made.start()
        self.copies.append(made)

    def start(self):
        link = self.link
        self.copy(0, self.whole.at[:, :, :, 1 - link.core], self.pair, link.over(1))

    def spread(self):
        link, half = self.link, self.half
        self.copies[0].wait_recv()

        def add(row):
            self.pair[row] = self.pair[row] + self.whole[row, :, :, link.core]

        loop(self.pair.shape[0], add)
        self.copy(1, self.pair.at[:, :, 1 - link.x, :, :half], self.first, link.over(2))
        self.copy(2, self.pair.at[:, 1 - link.y, :, :, half:], self.second, link.over(4))

    def cross(self):
        link, half = self.link, self.half
        self.copies[1].wait_recv()

        def add_first(row):
            self.first[row] = self.first[row] + self.pair[row, :, link.x, :, :half]

        loop(self.pair.shape[0], add_first)
        self.copy(3, self.first.at[:, 1 - link.y], self.plane.at[:, :, :half], link.over(4))
        self.copies[2].wait_recv()

        def add_second(row):
            self.second[row] = self.second[row] + self.pair[row, link.y, :, :, half:]

        loop(self.pair.shape[0], add_second)
        self.copy(4, self.second.at[:, 1 - link.x], self.plane.at[:, :, half:], link.over(2))

    def deal(self):
        link, half = self.link, self.half
        self.copies[3].wait_recv()
        self.copies[4].wait_recv()

        def add(row):
            self.plane[row, :, :half] = self.plane[row, :, :half] + self.first[row, link.y]
            self.plane[row, :, half:] = self.plane[row, :, half:] + self.second[row, link.x]

        loop(self.plane.shape[0], add)
        for step in range(1, link.lats):
            there = lax.rem(link.lat + step, link.lats)
            self.copy(4 + step, self.plane.at[there], self.slots.at[step - 1], (there, link.lon))

    def finish(self):
        link = self.link
        total = self.plane[link.lat].astype(F32)
        for step in range(1, link.lats):
            self.copies[4 + step].wait_recv()
            total = total + self.slots[step - 1].astype(F32)
        self.out[...] = total

    def drain(self):
        for made in self.copies:
            made.wait_send()


class Link:
    def __init__(self, lats, lons):
        self.lats, self.lons = lats, lons
        self.lat, self.lon = lax.axis_index("lat"), lax.axis_index("lon")
        self.core = lax.rem(self.lon, 2)
        self.x = lax.rem(self.lon // 2, 2)
        self.y = lax.rem(self.lon // 4, 2)

    def over(self, step):
        bit = lax.rem(self.lon // step, 2)
        return (self.lat, self.lon + step - 2 * step * bit)

    def at(self, north, west):
        return (
            lax.rem(self.lat + self.lats + north, self.lats),
            lax.rem(self.lon + self.lons + west, self.lons),
        )

    def greet(self):
        barrier = pltpu.get_barrier_semaphore()
        peers = [self.over(1), self.over(2), self.over(4)]
        peers += [self.at(step, 0) for step in range(1, self.lats)]
        peers += [self.at(0, 1), self.at(0, -1), self.at(1, 1), self.at(-1, -1)]
        for peer in peers:
            pl.semaphore_signal(barrier, inc=1, device_id=peer, device_id_type=pl.DeviceIdType.MESH)
        pl.semaphore_wait(barrier, len(peers))


def step_kernel(row_total, lats, lons, linked, names, *refs):
    r = types.SimpleNamespace(**dict(zip(names, refs)))
    main, marks = r.main, r.marks
    w_qkv, w_proj, w_fc1, w_fc2, w_head = r.w_qkv, r.w_proj, r.w_fc1, r.w_fc2, r.w_head
    latent, marks_win, normed1, qkv, probs = r.latent, r.marks_win, r.normed1, r.qkv, r.probs
    context, residual, normed2, activated = r.context, r.residual, r.normed2, r.activated
    slope, block_out, normed3, d_logits = r.slope, r.block_out, r.normed3, r.d_logits
    d_out, flipped, upper, lower = r.d_out, r.flipped, r.upper, r.lower
    strip = context
    row_count, col_count, width = main.shape
    total = row_count * col_count
    windows = total // TOKENS
    across = col_count // WIN_LON
    pairs = width // LANES
    block = row_block(total, 288)
    blocks = total // block
    wide = row_block(total, 448)
    wide_blocks = total // wide
    ff = w_fc1.shape[1]
    pitch = col_count + EDGE

    edge_copies = []
    if linked:
        link = Link(lats, lons)
        link.greet()

        def edge_copy(source, target, where):
            place = len(edge_copies)
            made = pltpu.make_async_remote_copy(
                src_ref=source, dst_ref=target, send_sem=r.edge_send.at[place],
                recv_sem=r.edge_recv.at[place], device_id=where,
                device_id_type=pl.DeviceIdType.MESH,
            )
            made.start()
            edge_copies.append(made)

        edges = (r.east, r.south, r.corner), (r.marks_east, r.marks_south, r.marks_corner)
        for grid, (east, south, corner) in zip((main, marks), edges):
            edge_copy(grid.at[:, : 2 * EDGE], east, link.at(0, -1))
            edge_copy(grid.at[:HALF_ROWS], south, link.at(-1, 0))
            edge_copy(grid.at[:HALF_ROWS, : 2 * EDGE], corner, link.at(-1, -1))
        sums = {
            name: Summed(link, [getattr(r, f"{name}{part}") for part in range(8)], getattr(r, "g_" + name))
            for name in GRADS
        }

    def advance(name, stage):
        if linked:
            stage(sums[name])

    def put(name, cols, value):
        if linked:
            whole = sums[name].whole
            whole[:, :, :, :, :, cols] = value.astype(BF16).reshape(*whole.shape[:5], TILE)
        else:
            getattr(r, "g_" + name)[:, cols] = value.astype(BF16)

    fill_table(upper, lower)
    for made in edge_copies:
        made.wait_recv()
    cut_windows(main, r.east, r.south, r.corner, strip, latent)
    cut_windows(marks, r.marks_east, r.marks_south, r.marks_corner, r.marks_strip, marks_win)

    def flip(source):
        for col in range(width // LANES):
            part = source[:total, col * LANES : (col + 1) * LANES]
            flipped[col * LANES : (col + 1) * LANES, :] = part.astype(BF16).T

    def weight_grad(name, right):
        def tile(place):
            put(name, cols_at(place), dot_nn(flipped[...], right[:, cols_at(place)].astype(BF16)))

        loop(right.shape[1] // TILE, tile)

    def first_norm(place):
        rows = rows_at(place, block)
        normed1[rows] = normalize(latent[rows])[0].astype(BF16)

    loop(blocks, first_norm)

    def project(place):
        qkv[:, cols_at(place)] = dot_nn(normed1[...], w_qkv[:, cols_at(place)])

    loop(3 * width // TILE, project)

    device_row = lax.axis_index("lat") * row_count + HALF_ROWS

    def units(place):
        return [(place * GROUP + part, pair) for part in range(GROUP) for pair in range(pairs)]

    def attend(place):
        place_q = lax.broadcasted_iota(jnp.int32, (TOKENS, TOKENS), 0)
        place_k = lax.broadcasted_iota(jnp.int32, (TOKENS, TOKENS), 1)
        bias = {}
        for part in range(GROUP):
            window = place * GROUP + part
            limit = (row_total - device_row - (window // across) * WIN_LAT) * WIN_LON
            alike = jnp.where((place_q >= limit) == (place_k >= limit), 0.0, masked)
            bias[part] = jnp.concatenate([alike, alike], 0)
        scores = []
        for index, (window, pair) in enumerate(units(place)):
            rows, start = rows_at(window, TOKENS), pair * LANES
            query = pair_stack(qkv[rows, start : start + LANES])
            key = qkv[rows, width + start : width + start + LANES].astype(BF16)
            scores.append(dot_nt(query, key) + bias[index // pairs])
        for score, (window, pair) in zip(scores, units(place)):
            exponent = jnp.exp2((score - jnp.max(score, -1, keepdims=True)) * SOFTMAX_SCALE)
            probs[window * pairs + pair] = exponent * (1.0 / jnp.sum(exponent, -1, keepdims=True))
        for window, pair in units(place):
            rows, start = rows_at(window, TOKENS), pair * LANES
            value = qkv[rows, 2 * width + start : 2 * width + start + LANES].astype(BF16)
            chance = probs[window * pairs + pair].astype(BF16)
            context[rows, start : start + LANES] = pair_merge(dot_nn(chance, value))

    loop(windows // GROUP, attend)

    def after_attention(place):
        rows = rows_at(place, block)
        attended = dot_nn(context[rows].astype(BF16), w_proj[...]).astype(BF16)
        summed = latent[rows] + attended.astype(F32)
        residual[rows] = summed
        normed2[rows] = normalize(summed)[0].astype(BF16)

    loop(blocks, after_attention)

    def widen(place):
        cols = cols_at(place // wide_blocks)
        rows = rows_at(place % wide_blocks, wide)
        pre_act = dot_nn(normed2[rows], w_fc1[:, cols])
        cdf = 0.5 * (1.0 + lax.erf(pre_act * (1.0 / math.sqrt(2.0))))
        density = jnp.exp2(pre_act * pre_act * (-0.5 / math.log(2.0))) * (1.0 / math.sqrt(2.0 * math.pi))
        activated[rows, cols] = (pre_act * cdf).astype(BF16)
        slope[rows, cols] = cdf + pre_act * density

    loop(wide_blocks * (ff // TILE), widen)

    def narrow(place):
        rows = rows_at(place, block)
        out = residual[rows] + dot_nn(activated[rows], w_fc2[...])
        block_out[rows] = out
        normed3[rows] = normalize(out)[0].astype(BF16)

    loop(blocks, narrow)

    def head(place):
        rows = rows_at(place, block)
        mark = marks_win[rows]
        weight_tok = mark[:, VARS : VARS + 1] / VARS
        bins = lax.broadcasted_iota(jnp.int32, (block, BINS), 1).astype(F32)
        for var in range(VARS):
            logits = dot_nn(normed3[rows], w_head[:, var * BINS : (var + 1) * BINS])
            exponent = jnp.exp(logits - jnp.max(logits, -1, keepdims=True))
            chance = exponent * (1.0 / jnp.sum(exponent, -1, keepdims=True))
            picked = jnp.where(mark[:, var : var + 1] == bins, 1.0, 0.0).astype(BF16)
            target = dot_nn(picked, upper[...]) + dot_nn(picked, lower[...])
            d_logits[rows, var * BINS : (var + 1) * BINS] = (weight_tok * (chance - target)).astype(BF16)

    loop(blocks, head)

    flip(normed3)
    weight_grad("head", d_logits)
    advance("head", Summed.start)
    d_outb = normed3

    def head_back(place):
        rows = rows_at(place, block)
        scaled, inverse = normalize(block_out[rows])
        back = norm_back(scaled, inverse, dot_nt(d_logits[rows], w_head[...]))
        d_out[rows] = back
        d_outb[rows] = back.astype(BF16)

    loop(blocks, head_back)
    advance("head", Summed.spread)

    fc2_rows = 4 * ff // (lats * lons) if linked else TILE

    def grad_narrow(place):
        grad = dot_nn(activated[:, cols_at(place, fc2_rows)].T, d_outb[...]).astype(BF16)
        if linked:
            whole = sums["fc2"].whole
            whole[place // 2, place % 2] = grad.reshape(*whole.shape[2:])
        else:
            r.g_fc2[rows_at(place, fc2_rows)] = grad

    loop(ff // fc2_rows, grad_narrow)
    advance("fc2", Summed.start)
    advance("head", Summed.cross)

    d_pre = slope

    def widen_back(place):
        cols = cols_at(place)
        back = dot_nt(d_outb[...], w_fc2[rows_at(place, TILE)])
        d_pre[:, cols] = back * slope[:, cols]

    loop(ff // TILE, widen_back)
    advance("fc2", Summed.spread)
    advance("head", Summed.deal)

    flip(normed2)
    weight_grad("fc1", d_pre)
    advance("fc1", Summed.start)

    d_attended = d_outb
    d_resid = d_out

    def residual_back(place):
        rows = rows_at(place, block)
        scaled, inverse = normalize(residual[rows])
        back = d_out[rows] + norm_back(scaled, inverse, dot_nt(d_pre[rows].astype(BF16), w_fc1[...]))
        d_resid[rows] = back
        d_attended[rows] = back.astype(BF16)

    loop(blocks, residual_back)
    advance("fc2", Summed.cross)
    advance("fc1", Summed.spread)

    flip(context)
    weight_grad("proj", d_attended)
    advance("proj", Summed.start)
    advance("head", Summed.finish)

    d_context = context

    def context_back(place):
        rows = rows_at(place, block)
        d_context[rows] = dot_nt(d_attended[rows], w_proj[...])

    loop(blocks, context_back)
    advance("fc2", Summed.deal)
    advance("proj", Summed.spread)

    def attend_back(place):
        d_probs = []
        for window, pair in units(place):
            rows, start = rows_at(window, TOKENS), pair * LANES
            upstream = pair_stack(d_context[rows, start : start + LANES])
            at_v = slice(2 * width + start, 2 * width + start + LANES)
            d_probs.append(dot_nt(upstream, qkv[rows, at_v].astype(BF16)))
            chance_t = probs[window * pairs + pair].T.astype(BF16)
            qkv[rows, at_v] = dot_nn(chance_t, upstream)
        for d_prob, (window, pair) in zip(d_probs, units(place)):
            rows, start = rows_at(window, TOKENS), pair * LANES
            at_q, at_k = slice(start, start + LANES), slice(width + start, width + start + LANES)
            query = pair_stack(qkv[rows, at_q])
            key = qkv[rows, at_k].astype(BF16)
            chance = probs[window * pairs + pair]
            inner = jnp.sum(d_prob * chance, -1, keepdims=True)
            d_scores = chance * (d_prob - inner) * HEAD_DIM ** (-0.5)
            qkv[rows, at_q] = pair_merge(dot_nn(d_scores.astype(BF16), key))
            qkv[rows, at_k] = dot_nn(d_scores.T.astype(BF16), query)

    def some_windows(first, last):
        loop(last - first, lambda window: attend_back(first + window))

    groups = windows // GROUP
    some_windows(0, groups // 3)
    advance("fc1", Summed.cross)
    some_windows(groups // 3, 2 * groups // 3)
    advance("proj", Summed.cross)
    advance("fc2", Summed.finish)
    advance("fc1", Summed.deal)
    advance("proj", Summed.deal)
    some_windows(2 * groups // 3, groups)

    flip(normed1)
    weight_grad("qkv", qkv)
    advance("qkv", Summed.start)
    advance("fc1", Summed.finish)
    advance("proj", Summed.finish)
    advance("qkv", Summed.spread)

    def latent_back(place):
        rows = rows_at(place, block)
        d_shifted = dot_nt(qkv[rows].astype(BF16), w_qkv[...]).astype(BF16)
        scaled, inverse = normalize(latent[rows])
        block_out[rows] = d_resid[rows] + norm_back(scaled, inverse, d_shifted.astype(F32))

    loop(blocks, latent_back)
    join_windows(block_out, strip, row_count, col_count)
    if not linked:
        for row in range(row_count):
            r.g_main[row] = strip[row * pitch : row * pitch + col_count].astype(BF16)
            r.g_edge[row] = strip[row * pitch + col_count : (row + 1) * pitch].astype(BF16)
        return

    own_rows = row_count - HALF_ROWS
    pad = jnp.zeros((EDGE, width), F32)
    for row in range(row_count):
        edge = jnp.concatenate([strip[row * pitch + col_count : (row + 1) * pitch], pad], 0)
        if row < own_rows:
            r.to_east[row] = edge.astype(BF16)
        else:
            r.to_corner[row - own_rows] = edge.astype(BF16)
            r.to_south[row - own_rows] = strip[row * pitch : row * pitch + col_count].astype(BF16)
    first_back = len(edge_copies)
    edge_copy(r.to_east, r.from_west, link.at(0, 1))
    edge_copy(r.to_south, r.from_north, link.at(1, 0))
    edge_copy(r.to_corner, r.from_corner, link.at(1, 1))
    advance("qkv", Summed.cross)

    ours = lax.broadcasted_iota(jnp.int32, (EDGE, width), 0) >= HALF_COLS

    def put_row(row, body, edge):
        head = jnp.where(ours, body[:EDGE], edge[:EDGE])
        r.g_main[row] = jnp.concatenate([head, body[EDGE:]], 0).astype(BF16)

    advance("qkv", Summed.deal)
    for made in edge_copies[first_back:]:
        made.wait_recv()
    for row in range(own_rows):
        body = strip[row * pitch : row * pitch + col_count]
        put_row(row + HALF_ROWS, body, r.from_west[row].astype(F32))
    for row in range(HALF_ROWS):
        put_row(row, r.from_north[row].astype(F32), r.from_corner[row].astype(F32))
    advance("qkv", Summed.finish)
    for made in edge_copies:
        made.wait_send()
    for name in GRADS:
        sums[name].drain()


GRADS = ("qkv", "proj", "fc1", "fc2", "head")


def device_step(latent, edges, marks, marks_edges, weights, lats, lons, linked):
    row_count, col_count, width = latent.shape
    total = row_count * col_count
    windows = total // TOKENS
    ff = weights[2].shape[1]
    lanes = marks.shape[-1]
    padded = row_count * (col_count + EDGE)
    w_qkv, w_proj, w_fc1, w_fc2, w_head = weights
    ins = dict(main=latent, marks=marks)
    if not linked:
        ins |= dict(zip(("east", "south", "corner"), edges))
        ins |= dict(zip(("marks_east", "marks_south", "marks_corner"), marks_edges))
    ins |= dict(w_qkv=w_qkv, w_proj=w_proj, w_fc1=w_fc1, w_fc2=w_fc2, w_head=w_head)
    outs = dict(g_main=jax.ShapeDtypeStruct((row_count, col_count, width), BF16))
    if not linked:
        outs |= dict(g_edge=jax.ShapeDtypeStruct((row_count, EDGE, width), BF16))
    for name, weight in zip(GRADS, weights):
        rows = weight.shape[0] // (lats * lons if linked else 1)
        outs["g_" + name] = jax.ShapeDtypeStruct((rows, weight.shape[1]), F32 if linked else BF16)
    scratch = dict(
        marks_strip=pltpu.VMEM((padded, lanes), F32),
        latent=pltpu.VMEM((total, width), F32),
        marks_win=pltpu.VMEM((total, lanes), F32),
        normed1=pltpu.VMEM((total, width), BF16),
        qkv=pltpu.VMEM((total, 3 * width), F32),
        probs=pltpu.VMEM((windows * (width // LANES), 2 * TOKENS, TOKENS), F32),
        context=pltpu.VMEM((padded, width), F32),
        residual=pltpu.VMEM((total, width), F32),
        normed2=pltpu.VMEM((total, width), BF16),
        activated=pltpu.VMEM((total, ff), BF16),
        slope=pltpu.VMEM((total, ff), F32),
        block_out=pltpu.VMEM((total, width), F32),
        normed3=pltpu.VMEM((total, width), BF16),
        d_logits=pltpu.VMEM((total, VARS * BINS), BF16),
        d_out=pltpu.VMEM((total, width), F32),
        flipped=pltpu.VMEM((width, total), BF16),
        upper=pltpu.VMEM((BINS, BINS), BF16),
        lower=pltpu.VMEM((BINS, BINS), BF16),
    )
    if linked:
        own_rows = row_count - HALF_ROWS
        wide, high, both = (row_count, 2 * EDGE), (HALF_ROWS, col_count), (HALF_ROWS, 2 * EDGE)
        own = (own_rows, 2 * EDGE)
        scratch |= dict(
            east=pltpu.VMEM((*wide, width), BF16),
            south=pltpu.VMEM((*high, width), BF16),
            corner=pltpu.VMEM((*both, width), BF16),
            marks_east=pltpu.VMEM((*wide, lanes), BF16),
            marks_south=pltpu.VMEM((*high, lanes), BF16),
            marks_corner=pltpu.VMEM((*both, lanes), BF16),
            to_east=pltpu.VMEM((*own, width), BF16),
            to_south=pltpu.VMEM((*high, width), BF16),
            to_corner=pltpu.VMEM((*both, width), BF16),
            from_west=pltpu.VMEM((*own, width), BF16),
            from_north=pltpu.VMEM((*high, width), BF16),
            from_corner=pltpu.VMEM((*both, width), BF16),
            edge_send=pltpu.SemaphoreType.DMA((9,)),
            edge_recv=pltpu.SemaphoreType.DMA((9,)),
        )
        for name, weight in zip(GRADS, weights):
            rows, cols = weight.shape[0] // (lats * lons), weight.shape[1]
            stages = [
                pltpu.VMEM((lats, 2, 2, 2, rows, cols), BF16),
                pltpu.VMEM((lats, 2, 2, rows, cols), BF16),
                pltpu.VMEM((lats, 2, rows, cols // 2), BF16),
                pltpu.VMEM((lats, 2, rows, cols // 2), BF16),
                pltpu.VMEM((lats, rows, cols), BF16),
                pltpu.VMEM((lats - 1, rows, cols), BF16),
                pltpu.SemaphoreType.DMA((4 + lats,)),
                pltpu.SemaphoreType.DMA((4 + lats,)),
            ]
            scratch |= {f"{name}{place}": stage for place, stage in enumerate(stages)}
    vmem = pl.BlockSpec(memory_space=pltpu.VMEM)
    names = [*ins, *outs, *scratch]
    done = pl.pallas_call(
        functools.partial(step_kernel, row_count * lats, lats, lons, linked, names),
        in_specs=[vmem] * len(ins),
        out_specs=[vmem] * len(outs),
        out_shape=list(outs.values()),
        scratch_shapes=list(scratch.values()),
        compiler_params=pltpu.CompilerParams(
            vmem_limit_bytes=67043328,
            **(dict(collective_id=0, has_side_effects=True) if linked else {}),
        ),
        cost_estimate=pl.CostEstimate(flops=20_000_000_000, bytes_accessed=20_000_000, transcendentals=0),
        name="device_step",
    )(*ins.values())
    return done


def moved(value, axis, steps):
    count = lax.axis_size(axis)
    pairs = [(source, (source + steps) % count) for source in range(count)]
    return lax.ppermute(value, axis, pairs)


def edges_ahead(block):
    east = moved(block[:, :EDGE], "lon", -1)
    south = moved(block[:HALF_ROWS], "lat", -1)
    return east, south, moved(east[:HALF_ROWS], "lat", -1)


def roll_behind(body, edge):
    own_rows = body.shape[0] - HALF_ROWS
    west = moved(edge, "lon", 1)[:, :HALF_COLS]
    whole = jnp.concatenate([west, body[:, HALF_COLS:]], 1)
    north = moved(whole[own_rows:], "lat", 1)
    return jnp.concatenate([north, whole[:own_rows]], 0)


def scatter_over(value, axis):
    return lax.psum_scatter(value, axis, scatter_dimension=0, tiled=True)


def local(latent, w_qkv, w_proj, w_fc1, w_fc2, w_head, target_bins, land_mask):
    width = latent.shape[2]
    lats, lons = lax.axis_size("lat"), lax.axis_size("lon")
    devices = lats * lons
    linked = lons == 8 and lats > 2 and width % (16 * devices) == 0
    marks = jnp.concatenate([target_bins, land_mask[:, :, None]], 2).astype(BF16)
    marks = jnp.pad(marks, ((0, 0), (0, 0), (0, LANES - marks.shape[2])))
    weights = (w_qkv, w_proj, w_fc1, w_fc2, w_head)
    if linked:
        return tuple(device_step(latent, (), marks, (), weights, lats, lons, True))
    body, edge, *grads = device_step(
        latent, edges_ahead(latent), marks, edges_ahead(marks), weights, lats, lons, False
    )
    grad_latent = roll_behind(body, edge)

    def to_columns(grad):
        deep = grad.shape[0] // width
        parts = grad.reshape(devices, deep, width // devices, -1)
        return [parts[:, part].reshape(width, -1) for part in range(deep)]

    columns = [to_columns(grad) for grad in grads]
    joined = jnp.concatenate([part for group in columns for part in group], 1)
    summed = scatter_over(scatter_over(joined, "lat"), "lon").astype(F32)
    outs, start = [], 0
    for grad, group in zip(grads, columns):
        size = grad.shape[1]
        pieces = [summed[:, start + part * size : start + (part + 1) * size] for part in range(len(group))]
        outs.append(jnp.concatenate(pieces, 0))
        start += size * len(group)
    return (grad_latent, *outs)


def solution(mesh):
    grid = P("lat", "lon", None)
    spread = P(("lat", "lon"), None)
    return jax.shard_map(
        local,
        mesh=mesh,
        in_specs=(grid, P(), P(), P(), P(), P(), grid, P("lat", "lon")),
        out_specs=(grid, spread, spread, spread, spread, spread),
        check_vma=False,
    )
```

time: 362 us -> 111 us (0.31)
  waiting for transfers between devices: 172 us -> 0 us
  matrix products: 59.3 us -> 0 us
  Pallas kernels: 48.4 us -> 100 us
  local copies, waits for them, and re-layouts: 33.3 us -> 7.45 us
  other arithmetic: 20.1 us -> 2.29 us
  between operations: 14.3 us -> 0.68 us
  starting transfers between devices: 13.6 us -> 0 us
    reduce_scatter x3 -> x0, waiting for transfers between devices: 155 us -> none  [scatter_over(): return lax.psum_scatter(value, axis, scatter_dimension=0, tiled=True)]
    dot_general x26 -> x0, matrix products: 59.3 us -> none  [the longest x4 5.12 us: head_grad(): jnp.dot(picked, upper, preferred_element_type=jnp.float32)]
    pallas_call x2 -> x1, Pallas kernels: 48.4 us -> 100 us  [device_step(): pl.pallas_call(functools.partial(step_kernel, row_count * lats, lats, lon...]
    ppermute x6 -> x0, waiting for transfers between devices: 15.9 us -> none  [shifted_2(): return lax.ppermute(value, axis, pairs)]
    ppermute x6 -> x0, starting transfers between devices: 13.4 us -> none  [shifted_2(): return lax.ppermute(value, axis, pairs)]
    convert_element_type x5 -> x0, local copies, waits for them, and re-layouts: 11.3 us -> none  [the longest x3 8.76 us: local(): residual_in = to_windows(roll_ahead(latent)).astype(jnp.float32)]
    slice x9 -> x0, local copies, waits for them, and re-layouts: 7.71 us -> none  [the longest x1 1.54 us: local(): sum_fc2 = early[:, third:].reshape(-1, ratio, feat_width).transpose(1, 0, 2)]
    convert_element_type x9 -> x0, other arithmetic: 6.78 us -> none  [the longest x1 1.76 us: local(): d_attended = d_resid.astype(jnp.bfloat16)]
  transfers between devices with their start and end apart: 9 -> 0, of which waited for: 7 -> 0; matrix products, arithmetic and copies ran while one was open for 6% -> 0% of each run, Pallas kernels for 0% -> 0%
where the time goes in v1:
time: 111 us
  Pallas kernels  100 us (90%)
  local copies, waits for them, and re-layouts  7.45 us (7%)
  other arithmetic  2.29 us (2%)
    pallas_call x1, Pallas kernels, device_step(): pl.pallas_call(functools.partial(step_kernel, row_count * lats, lats, lon...  100 us
    unnamed x12, local copies, waits for them, and re-layouts  7.05 us

profile of v1, /device:TPU:0, one launch (start us, length us, event | category | flops | bytes accessed | tf_op | source)
XLA Modules:
  0.0 110.7 jit_solution(6959347843357254108)
XLA Ops:
  0.6 0.7 convert_bitcast_fusion
  1.3 0.7 convert.7
  2.1 0.2 copy.21
  2.3 0.2 copy.22
  2.5 0.8 fusion.2.refs_1_
  3.3 100.3 %device_step.1 = (bf16[12,72,512]{2,1,0:T(8,128)(2,1)}, f32[16,1536]{1,0:T(8,128)}, f32[16,512]{1,0:T(8,128)}, f32[16,2048]{1,0:T(8,128)}, f32[64,512]{1,0:T(8,128)}, /*index=5*/f32[16,1024]{1,0:T(8,128)}) custom-call(bf16[12,72,512]{2,1,0:T(8,128)(2,1)} %refs_0_.1, bf16[12,72,128]{2,1,0:T(8,128)(2,1)} %fusion.2.refs_1_, bf16[512,1536]{1,0:T(8,128)(2,1)} %refs_2_.1, ...), custom_call_target="tpu_custom_call" | custom-call | flops 20000000000 | bytes 20000000 | tf_op jit(solution)/shard_map/device_step/pallas_call | solution.py:642
  103.6 0.0 copy-start.1
  103.6 0.0 copy-start
  103.6 0.0 copy-start.2
  103.6 2.2 %copy.29 = bf16[12,72,512]{2,1,0:T(8,128)(2,1)} copy(bf16[12,72,512]{2,1,0:T(8,128)(2,1)} %get-tuple-element.12) | data formatting | bytes 1769472
  105.8 1.5 %copy.30 = f32[16,1536]{1,0:T(8,128)} copy(f32[16,1536]{1,0:T(8,128)} %get-tuple-element.13) | data formatting | bytes 196608
  107.4 1.4 %copy.31 = f32[16,512]{1,0:T(8,128)} copy(f32[16,512]{1,0:T(8,128)} %get-tuple-element.14) | data formatting | bytes 65536
  108.7 0.0 copy-done.1
  108.7 0.7 copy.32
  109.4 0.0 copy-done
  109.4 0.7 copy.33
  110.0 0.0 copy-done.2
  110.0 0.6 copy.34
Async XLA Ops:
  103.6 5.1 %copy-start.1 = (f32[16,2048]{1,0:T(8,128)S(1)}, f32[16,2048]{1,0:T(8,128)}, u32[]{:S(2)}) copy-start(f32[16,2048]{1,0:T(8,128)} %get-tuple-element.15) | copy-start | bytes 393220
  103.6 5.8 %copy-start = (f32[64,512]{1,0:T(8,128)S(1)}, f32[64,512]{1,0:T(8,128)}, u32[]{:S(2)}) copy-start(f32[64,512]{1,0:T(8,128)} %get-tuple-element.16) | copy-start | bytes 393220
  103.6 6.4 %copy-start.2 = (f32[16,1024]{1,0:T(8,128)S(1)}, f32[16,1024]{1,0:T(8,128)}, u32[]{:S(2)}) copy-start(f32[16,1024]{1,0:T(8,128)} %get-tuple-element.17) | copy-start | bytes 196612

commit v2 on v1

--- a/solution.py
+++ b/solution.py
@@ -26,7 +26,7 @@
 smear = 0.75
 masked = -1e30
 SOFTMAX_SCALE = HEAD_DIM ** (-0.5) / math.log(2.0)
-GROUP = 2
+
 F32 = jnp.float32
 BF16 = jnp.bfloat16
 
@@ -90,20 +90,20 @@
     return jnp.where(lane < HEAD_DIM, top, bottom)
 
 
-def cut_windows(main, east, south, corner, strip, wins):
+def cut_windows(part, main, east, south, corner, strip, wins):
     row_count, col_count = main.shape[0], main.shape[1]
     own_rows = row_count - HALF_ROWS
     across, pitch = col_count // WIN_LON, col_count + EDGE
-    for row in range(row_count):
+    for row in range(part * WIN_LAT, (part + 1) * WIN_LAT):
         if row < own_rows:
             body, edge = main[row + HALF_ROWS], east[row + HALF_ROWS]
         else:
             body, edge = south[row - own_rows], corner[row - own_rows]
         strip[row * pitch : row * pitch + col_count] = body.astype(F32)
         strip[row * pitch + col_count : (row + 1) * pitch] = edge.astype(F32)[:EDGE]
-    for row in range(row_count):
+    for row in range(part * WIN_LAT, (part + 1) * WIN_LAT):
         for col in range(across):
-            start = ((row // WIN_LAT) * across + col) * TOKENS + (row % WIN_LAT) * WIN_LON
+            start = (part * across + col) * TOKENS + (row % WIN_LAT) * WIN_LON
             first = row * pitch + HALF_COLS + col * WIN_LON
             wins[start : start + WIN_LON] = strip[first : first + WIN_LON]
 
@@ -243,17 +243,25 @@
 def step_kernel(row_total, lats, lons, linked, names, *refs):
     r = types.SimpleNamespace(**dict(zip(names, refs)))
     main, marks = r.main, r.marks
-    w_qkv, w_proj, w_fc1, w_fc2, w_head = r.w_qkv, r.w_proj, r.w_fc1, r.w_fc2, r.w_head
+    w_qkv, w_proj, w_fc1, w_fc2, w_head = (getattr(r, f"held{place}") for place in range(5))
+    arrivals = [
+        pltpu.make_async_copy(getattr(r, f"weight{place}"), getattr(r, f"held{place}"), r.weight_sem.at[place])
+        for place in range(5)
+    ]
+    for place in (0, 1, 2, 3, 4):
+        arrivals[place].start()
     latent, marks_win, normed1, qkv, probs = r.latent, r.marks_win, r.normed1, r.qkv, r.probs
     context, residual, normed2, activated = r.context, r.residual, r.normed2, r.activated
     slope, block_out, normed3, d_logits = r.slope, r.block_out, r.normed3, r.d_logits
     d_out, flipped, upper, lower = r.d_out, r.flipped, r.upper, r.lower
     strip = context
+    strip_in = r.residual
     row_count, col_count, width = main.shape
     total = row_count * col_count
     windows = total // TOKENS
     across = col_count // WIN_LON
     pairs = width // LANES
+    group = 2 - across % 2
     block = row_block(total, 288)
     blocks = total // block
     wide = row_block(total, 448)
@@ -276,11 +284,9 @@
             made.start()
             edge_copies.append(made)
 
-        edges = (r.east, r.south, r.corner), (r.marks_east, r.marks_south, r.marks_corner)
-        for grid, (east, south, corner) in zip((main, marks), edges):
-            edge_copy(grid.at[:, : 2 * EDGE], east, link.at(0, -1))
-            edge_copy(grid.at[:HALF_ROWS], south, link.at(-1, 0))
-            edge_copy(grid.at[:HALF_ROWS, : 2 * EDGE], corner, link.at(-1, -1))
+        edge_copy(main.at[:, : 2 * EDGE], r.east, link.at(0, -1))
+        edge_copy(main.at[:HALF_ROWS], r.south, link.at(-1, 0))
+        edge_copy(main.at[:HALF_ROWS, : 2 * EDGE], r.corner, link.at(-1, -1))
         sums = {
             name: Summed(link, [getattr(r, f"{name}{part}") for part in range(8)], getattr(r, "g_" + name))
             for name in GRADS
@@ -297,11 +303,23 @@
         else:
             getattr(r, "g_" + name)[:, cols] = value.astype(BF16)
 
+    def arrived(*places):
+        for place in places:
+            if linked:
+                edge_copies[place].wait_recv()
+
+    def fill_marks(row):
+        pad = jnp.zeros((8 - VARS - 1, col_count), F32)
+        bins, land = r.target[row].astype(F32), r.land[row : row + 1].astype(F32)
+        marks[row, :, :8] = jnp.concatenate([bins, land, pad], 0).T
+
+    for row in range(row_count):
+        fill_marks(row)
+    if linked:
+        edge_copy(marks.at[:, :EDGE], r.marks_east, link.at(0, -1))
+        edge_copy(marks.at[:HALF_ROWS], r.marks_south, link.at(-1, 0))
+        edge_copy(marks.at[:HALF_ROWS, :EDGE], r.marks_corner, link.at(-1, -1))
     fill_table(upper, lower)
-    for made in edge_copies:
-        made.wait_recv()
-    cut_windows(main, r.east, r.south, r.corner, strip, latent)
-    cut_windows(marks, r.marks_east, r.marks_south, r.marks_corner, r.marks_strip, marks_win)
 
     def flip(source):
         for col in range(width // LANES):
@@ -314,28 +332,17 @@
 
         loop(right.shape[1] // TILE, tile)
 
-    def first_norm(place):
-        rows = rows_at(place, block)
-        normed1[rows] = normalize(latent[rows])[0].astype(BF16)
-
-    loop(blocks, first_norm)
-
-    def project(place):
-        qkv[:, cols_at(place)] = dot_nn(normed1[...], w_qkv[:, cols_at(place)])
-
-    loop(3 * width // TILE, project)
-
     device_row = lax.axis_index("lat") * row_count + HALF_ROWS
 
     def units(place):
-        return [(place * GROUP + part, pair) for part in range(GROUP) for pair in range(pairs)]
+        return [(place * group + part, pair) for part in range(group) for pair in range(pairs)]
 
     def attend(place):
         place_q = lax.broadcasted_iota(jnp.int32, (TOKENS, TOKENS), 0)
         place_k = lax.broadcasted_iota(jnp.int32, (TOKENS, TOKENS), 1)
         bias = {}
-        for part in range(GROUP):
-            window = place * GROUP + part
+        for part in range(group):
+            window = place * group + part
             limit = (row_total - device_row - (window // across) * WIN_LAT) * WIN_LON
             alike = jnp.where((place_q >= limit) == (place_k >= limit), 0.0, masked)
             bias[part] = jnp.concatenate([alike, alike], 0)
@@ -354,7 +361,31 @@
             chance = probs[window * pairs + pair].astype(BF16)
             context[rows, start : start + LANES] = pair_merge(dot_nn(chance, value))
 
-    loop(windows // GROUP, attend)
+    half = across * TOKENS
+    half_block = row_block(half, 288)
+
+    def first_norm(place):
+        rows = rows_at(place, half_block)
+        normed1[rows] = normalize(latent[rows])[0].astype(BF16)
+
+    def project(part, place):
+        rows = slice(part * half, (part + 1) * half)
+        qkv[rows, cols_at(place)] = dot_nn(normed1[rows], w_qkv[:, cols_at(place)])
+
+    parts = row_count // WIN_LAT
+    for part in range(parts):
+        if part == 0:
+            arrived(0)
+        if part == parts - 1:
+            arrived(1, 2)
+        cut_windows(part, main, r.east, r.south, r.corner, strip_in, latent)
+        steps = half // half_block
+        loop(steps, lambda place: first_norm(part * steps + place))
+        if part == 0:
+            arrivals[0].wait()
+        loop(3 * width // TILE, lambda place: project(part, place))
+        groups = across // group
+        loop(groups, lambda place: attend(part * groups + place))
 
     def after_attention(place):
         rows = rows_at(place, block)
@@ -363,6 +394,7 @@
         residual[rows] = summed
         normed2[rows] = normalize(summed)[0].astype(BF16)
 
+    arrivals[1].wait()
     loop(blocks, after_attention)
 
     def widen(place):
@@ -374,6 +406,7 @@
         activated[rows, cols] = (pre_act * cdf).astype(BF16)
         slope[rows, cols] = cdf + pre_act * density
 
+    arrivals[2].wait()
     loop(wide_blocks * (ff // TILE), widen)
 
     def narrow(place):
@@ -382,6 +415,7 @@
         block_out[rows] = out
         normed3[rows] = normalize(out)[0].astype(BF16)
 
+    arrivals[3].wait()
     loop(blocks, narrow)
 
     def head(place):
@@ -397,6 +431,10 @@
             target = dot_nn(picked, upper[...]) + dot_nn(picked, lower[...])
             d_logits[rows, var * BINS : (var + 1) * BINS] = (weight_tok * (chance - target)).astype(BF16)
 
+    arrived(3, 4, 5)
+    for part in range(parts):
+        cut_windows(part, marks, r.marks_east, r.marks_south, r.marks_corner, r.marks_strip, marks_win)
+    arrivals[4].wait()
     loop(blocks, head)
 
     flip(normed3)
@@ -469,7 +507,6 @@
         d_context[rows] = dot_nt(d_attended[rows], w_proj[...])
 
     loop(blocks, context_back)
-    advance("fc2", Summed.deal)
     advance("proj", Summed.spread)
 
     def attend_back(place):
@@ -495,22 +532,17 @@
     def some_windows(first, last):
         loop(last - first, lambda window: attend_back(first + window))
 
-    groups = windows // GROUP
+    groups = windows // group
     some_windows(0, groups // 3)
+    advance("fc2", Summed.deal)
+    some_windows(groups // 3, groups)
     advance("fc1", Summed.cross)
-    some_windows(groups // 3, 2 * groups // 3)
-    advance("proj", Summed.cross)
-    advance("fc2", Summed.finish)
-    advance("fc1", Summed.deal)
-    advance("proj", Summed.deal)
-    some_windows(2 * groups // 3, groups)
 
     flip(normed1)
     weight_grad("qkv", qkv)
     advance("qkv", Summed.start)
-    advance("fc1", Summed.finish)
-    advance("proj", Summed.finish)
-    advance("qkv", Summed.spread)
+    advance("proj", Summed.cross)
+    advance("fc2", Summed.finish)
 
     def latent_back(place):
         rows = rows_at(place, block)
@@ -519,6 +551,8 @@
         block_out[rows] = d_resid[rows] + norm_back(scaled, inverse, d_shifted.astype(F32))
 
     loop(blocks, latent_back)
+    advance("qkv", Summed.spread)
+    advance("fc1", Summed.deal)
     join_windows(block_out, strip, row_count, col_count)
     if not linked:
         for row in range(row_count):
@@ -539,8 +573,10 @@
     edge_copy(r.to_east, r.from_west, link.at(0, 1))
     edge_copy(r.to_south, r.from_north, link.at(1, 0))
     edge_copy(r.to_corner, r.from_corner, link.at(1, 1))
+
+    advance("proj", Summed.deal)
     advance("qkv", Summed.cross)
-
+    advance("fc1", Summed.finish)
     ours = lax.broadcasted_iota(jnp.int32, (EDGE, width), 0) >= HALF_COLS
 
     def put_row(row, body, edge):
@@ -555,6 +591,7 @@
         put_row(row + HALF_ROWS, body, r.from_west[row].astype(F32))
     for row in range(HALF_ROWS):
         put_row(row, r.from_north[row].astype(F32), r.from_corner[row].astype(F32))
+    advance("proj", Summed.finish)
     advance("qkv", Summed.finish)
     for made in edge_copies:
         made.wait_send()
@@ -565,34 +602,36 @@
 GRADS = ("qkv", "proj", "fc1", "fc2", "head")
 
 
-def device_step(latent, edges, marks, marks_edges, weights, lats, lons, linked):
+def device_step(latent, edges, target, land, marks_edges, weights, lats, lons, linked):
     row_count, col_count, width = latent.shape
     total = row_count * col_count
     windows = total // TOKENS
     ff = weights[2].shape[1]
-    lanes = marks.shape[-1]
     padded = row_count * (col_count + EDGE)
-    w_qkv, w_proj, w_fc1, w_fc2, w_head = weights
-    ins = dict(main=latent, marks=marks)
+    ins = dict(main=latent, target=target.transpose(0, 2, 1), land=land)
     if not linked:
         ins |= dict(zip(("east", "south", "corner"), edges))
         ins |= dict(zip(("marks_east", "marks_south", "marks_corner"), marks_edges))
-    ins |= dict(w_qkv=w_qkv, w_proj=w_proj, w_fc1=w_fc1, w_fc2=w_fc2, w_head=w_head)
+    near = len(ins)
+    ins |= {f"weight{place}": weight for place, weight in enumerate(weights)}
     outs = dict(g_main=jax.ShapeDtypeStruct((row_count, col_count, width), BF16))
     if not linked:
         outs |= dict(g_edge=jax.ShapeDtypeStruct((row_count, EDGE, width), BF16))
     for name, weight in zip(GRADS, weights):
         rows = weight.shape[0] // (lats * lons if linked else 1)
         outs["g_" + name] = jax.ShapeDtypeStruct((rows, weight.shape[1]), F32 if linked else BF16)
-    scratch = dict(
-        marks_strip=pltpu.VMEM((padded, lanes), F32),
+    scratch = {f"held{place}": pltpu.VMEM(weight.shape, BF16) for place, weight in enumerate(weights)}
+    scratch |= dict(
+        weight_sem=pltpu.SemaphoreType.DMA((len(weights),)),
+        marks=pltpu.VMEM((row_count, col_count, LANES), F32),
+        marks_strip=pltpu.VMEM((padded, LANES), F32),
         latent=pltpu.VMEM((total, width), F32),
-        marks_win=pltpu.VMEM((total, lanes), F32),
+        marks_win=pltpu.VMEM((total, LANES), F32),
         normed1=pltpu.VMEM((total, width), BF16),
         qkv=pltpu.VMEM((total, 3 * width), F32),
         probs=pltpu.VMEM((windows * (width // LANES), 2 * TOKENS, TOKENS), F32),
         context=pltpu.VMEM((padded, width), F32),
-        residual=pltpu.VMEM((total, width), F32),
+        residual=pltpu.VMEM((padded, width), F32),
         normed2=pltpu.VMEM((total, width), BF16),
         activated=pltpu.VMEM((total, ff), BF16),
         slope=pltpu.VMEM((total, ff), F32),
@@ -612,9 +651,9 @@
             east=pltpu.VMEM((*wide, width), BF16),
             south=pltpu.VMEM((*high, width), BF16),
             corner=pltpu.VMEM((*both, width), BF16),
-            marks_east=pltpu.VMEM((*wide, lanes), BF16),
-            marks_south=pltpu.VMEM((*high, lanes), BF16),
-            marks_corner=pltpu.VMEM((*both, lanes), BF16),
+            marks_east=pltpu.VMEM((row_count, EDGE, LANES), F32),
+            marks_south=pltpu.VMEM((*high, LANES), F32),
+            marks_corner=pltpu.VMEM((HALF_ROWS, EDGE, LANES), F32),
             to_east=pltpu.VMEM((*own, width), BF16),
             to_south=pltpu.VMEM((*high, width), BF16),
             to_corner=pltpu.VMEM((*both, width), BF16),
@@ -641,7 +680,7 @@
     names = [*ins, *outs, *scratch]
     done = pl.pallas_call(
         functools.partial(step_kernel, row_count * lats, lats, lons, linked, names),
-        in_specs=[vmem] * len(ins),
+        in_specs=[vmem] * near + [pl.BlockSpec(memory_space=pl.ANY)] * len(weights),
         out_specs=[vmem] * len(outs),
         out_shape=list(outs.values()),
         scratch_shapes=list(scratch.values()),
@@ -652,7 +691,23 @@
         cost_estimate=pl.CostEstimate(flops=20_000_000_000, bytes_accessed=20_000_000, transcendentals=0),
         name="device_step",
     )(*ins.values())
-    return done
+    return settled(done) if linked else done
+
+
+def settle_kernel(count, *refs):
+    for source, target in zip(refs[:count], refs[count:]):
+        target[...] = source[...]
+
+
+def settled(arrays):
+    vmem = pl.BlockSpec(memory_space=pltpu.VMEM)
+    return pl.pallas_call(
+        functools.partial(settle_kernel, len(arrays)),
+        in_specs=[vmem] * len(arrays),
+        out_specs=[vmem] * len(arrays),
+        out_shape=[jax.ShapeDtypeStruct(array.shape, array.dtype) for array in arrays],
+        name="settle",
+    )(*arrays)
 
 
 def moved(value, axis, steps):
@@ -684,13 +739,13 @@
     lats, lons = lax.axis_size("lat"), lax.axis_size("lon")
     devices = lats * lons
     linked = lons == 8 and lats > 2 and width % (16 * devices) == 0
-    marks = jnp.concatenate([target_bins, land_mask[:, :, None]], 2).astype(BF16)
-    marks = jnp.pad(marks, ((0, 0), (0, 0), (0, LANES - marks.shape[2])))
     weights = (w_qkv, w_proj, w_fc1, w_fc2, w_head)
     if linked:
-        return tuple(device_step(latent, (), marks, (), weights, lats, lons, True))
+        return tuple(device_step(latent, (), target_bins, land_mask, (), weights, lats, lons, True))
+    marks = jnp.concatenate([target_bins, land_mask[:, :, None]], 2).astype(F32)
+    marks = jnp.pad(marks, ((0, 0), (0, 0), (0, LANES - marks.shape[2])))
     body, edge, *grads = device_step(
-        latent, edges_ahead(latent), marks, edges_ahead(marks), weights, lats, lons, False
+        latent, edges_ahead(latent), target_bins, land_mask, edges_ahead(marks), weights, lats, lons, False
     )
     grad_latent = roll_behind(body, edge)
 

time: 111 us -> 93.7 us (0.84)
  local copies, waits for them, and re-layouts: 7.45 us -> 0 us
  Pallas kernels: 100 us -> 92.9 us
  other arithmetic: 2.29 us -> 0 us
    pallas_call x1, Pallas kernels: 100 us -> 90.6 us  [device_step(): pl.pallas_call(functools.partial(step_kernel, row_count * lats, lats, lon...]
    unnamed x12 -> x0, local copies, waits for them, and re-layouts: 7.05 us -> none
    pallas_call x0 -> x1, Pallas kernels: none -> 2.37 us  [settled(): pl.pallas_call(functools.partial(settle_kernel, len(arrays)), in_specs=[v...]
where the time goes in v2:
time: 93.7 us; the launch traced here: 93.6 us
  Pallas kernels  92.9 us (99%)
    pallas_call x1, Pallas kernels, device_step(): pl.pallas_call(functools.partial(step_kernel, row_count * lats, lats, lon...  90.6 us
    pallas_call x1, Pallas kernels, settled(): pl.pallas_call(functools.partial(settle_kernel, len(arrays)), in_specs=[v...  2.37 us

profile of v2, /device:TPU:0, one launch (start us, length us, event | category | flops | bytes accessed | tf_op | source)
XLA Modules:
  0.0 93.6 jit_solution(4083726238430383597)
XLA Ops:
  0.6 90.6 %device_step.1 = (bf16[12,72,512]{2,1,0:T(8,128)(2,1)}, f32[16,1536]{1,0:T(8,128)}, f32[16,512]{1,0:T(8,128)}, f32[16,2048]{1,0:T(8,128)}, f32[64,512]{1,0:T(8,128)}, /*index=5*/f32[16,1024]{1,0:T(8,128)}) custom-call(bf16[12,72,512]{2,1,0:T(8,128)(2,1)} %refs_0_.1, s32[12,4,72]{2,1,0:T(4,128)} %bitcast.1, s32[12,72]{1,0:T(8,128)} %refs_2_.1, ...), custom_call_target="tpu_custom_call" | custom-call | flops 20000000000 | bytes 20000000 | tf_op jit(solution)/shard_map/device_step/pallas_call | solution.py:681
  91.2 2.4 %settle.1 = (bf16[12,72,512]{2,1,0:T(8,128)(2,1)}, f32[16,1536]{1,0:T(8,128)}, f32[16,512]{1,0:T(8,128)}, f32[16,2048]{1,0:T(8,128)}, f32[64,512]{1,0:T(8,128)}, /*index=5*/f32[16,1024]{1,0:T(8,128)}) custom-call(bf16[12,72,512]{2,1,0:T(8,128)(2,1)} %get-tuple-element.12.refs_0_, f32[16,1536]{1,0:T(8,128)} %get-tuple-element.13.refs_1_, ...), custom_call_target="tpu_custom_call" | custom-call | tf_op jit(solution)/shard_map/settle/pallas_call | solution.py:704

commit v3 on v2

--- a/solution.py
+++ b/solution.py
@@ -62,6 +62,10 @@
     lax.fori_loop(0, count, step, 0)
 
 
+def loop_from(first, last, body):
+    loop(last - first, lambda place: body(first + place))
+
+
 def rows_at(place, size):
     return pl.ds(pl.multiple_of(place * size, math.gcd(size, 16)), size)
 
@@ -90,31 +94,36 @@
     return jnp.where(lane < HEAD_DIM, top, bottom)
 
 
-def cut_windows(part, main, east, south, corner, strip, wins):
+def lay_rows(rows, main, east, south, corner, strip, bodies, edges):
     row_count, col_count = main.shape[0], main.shape[1]
-    own_rows = row_count - HALF_ROWS
+    own_rows, pitch = row_count - HALF_ROWS, col_count + EDGE
+    for row in rows:
+        if row < own_rows:
+            body, edge = main.at[row + HALF_ROWS], east.at[row]
+        else:
+            body, edge = south.at[row - own_rows], corner.at[row - own_rows]
+        if bodies:
+            strip[row * pitch : row * pitch + col_count] = body[...].astype(F32)
+        if edges:
+            strip[row * pitch + col_count : (row + 1) * pitch] = edge[...].astype(F32)[:EDGE]
+
+
+def cut_windows(first, last, col_count, strip, wins):
+    across, pitch = col_count // WIN_LON, col_count + EDGE
+    for window in range(first, last):
+        for row in range(WIN_LAT):
+            start = window * TOKENS + row * WIN_LON
+            source = (window // across * WIN_LAT + row) * pitch + HALF_COLS + window % across * WIN_LON
+            wins[start : start + WIN_LON] = strip[source : source + WIN_LON]
+
+
+def join_windows(part, wins, strip, col_count):
     across, pitch = col_count // WIN_LON, col_count + EDGE
     for row in range(part * WIN_LAT, (part + 1) * WIN_LAT):
-        if row < own_rows:
-            body, edge = main[row + HALF_ROWS], east[row + HALF_ROWS]
-        else:
-            body, edge = south[row - own_rows], corner[row - own_rows]
-        strip[row * pitch : row * pitch + col_count] = body.astype(F32)
-        strip[row * pitch + col_count : (row + 1) * pitch] = edge.astype(F32)[:EDGE]
-    for row in range(part * WIN_LAT, (part + 1) * WIN_LAT):
         for col in range(across):
-            start = (part * across + col) * TOKENS + (row % WIN_LAT) * WIN_LON
-            first = row * pitch + HALF_COLS + col * WIN_LON
-            wins[start : start + WIN_LON] = strip[first : first + WIN_LON]
-
-
-def join_windows(wins, strip, row_count, col_count):
-    across, pitch = col_count // WIN_LON, col_count + EDGE
-    for row in range(row_count):
-        for col in range(across):
-            start = ((row // WIN_LAT) * across + col) * TOKENS + (row % WIN_LAT) * WIN_LON
-            first = row * pitch + HALF_COLS + col * WIN_LON
-            strip[first : first + WIN_LON] = wins[start : start + WIN_LON]
+            start = (part * across + col) * TOKENS + row % WIN_LAT * WIN_LON
+            target = row * pitch + HALF_COLS + col * WIN_LON
+            strip[target : target + WIN_LON] = wins[start : start + WIN_LON]
 
 
 def fill_table(upper, lower):
@@ -137,8 +146,8 @@
 
 
 class Summed:
-    def __init__(self, link, refs, out):
-        self.link, self.out = link, out
+    def __init__(self, link, refs, out, cols):
+        self.link, self.out, self.cols = link, out, cols
         self.whole, self.pair, self.first, self.second, self.plane, self.slots = refs[:6]
         self.semaphores = refs[6:]
         self.half = self.plane.shape[-1] // 2
@@ -205,7 +214,7 @@
         for step in range(1, link.lats):
             self.copies[4 + step].wait_recv()
             total = total + self.slots[step - 1].astype(F32)
-        self.out[...] = total
+        self.out[:, self.cols] = total
 
     def drain(self):
         for made in self.copies:
@@ -254,8 +263,8 @@
     context, residual, normed2, activated = r.context, r.residual, r.normed2, r.activated
     slope, block_out, normed3, d_logits = r.slope, r.block_out, r.normed3, r.d_logits
     d_out, flipped, upper, lower = r.d_out, r.flipped, r.upper, r.lower
-    strip = context
     strip_in = r.residual
+    strip_out = r.strip_out
     row_count, col_count, width = main.shape
     total = row_count * col_count
     windows = total // TOKENS
@@ -269,7 +278,7 @@
     ff = w_fc1.shape[1]
     pitch = col_count + EDGE
 
-    edge_copies = []
+    edge_copies, sums = [], {}
     if linked:
         link = Link(lats, lons)
         link.greet()
@@ -284,24 +293,19 @@
             made.start()
             edge_copies.append(made)
 
-        edge_copy(main.at[:, : 2 * EDGE], r.east, link.at(0, -1))
+        edge_copy(main.at[:HALF_ROWS, : 2 * EDGE], r.corner, link.at(-1, -1))
         edge_copy(main.at[:HALF_ROWS], r.south, link.at(-1, 0))
-        edge_copy(main.at[:HALF_ROWS, : 2 * EDGE], r.corner, link.at(-1, -1))
-        sums = {
-            name: Summed(link, [getattr(r, f"{name}{part}") for part in range(8)], getattr(r, "g_" + name))
-            for name in GRADS
-        }
-
-    def advance(name, stage):
+        edge_copy(main.at[HALF_ROWS:, : 2 * EDGE], r.east, link.at(0, -1))
+        for name, parts in GRADS:
+            out = getattr(r, "g_" + name)
+            for part in range(parts):
+                size = out.shape[1] // parts
+                refs = [getattr(r, f"{name}{part}_{place}") for place in range(8)]
+                sums[name, part] = Summed(link, refs, out, slice(part * size, (part + 1) * size))
+
+    def advance(name, part, stage):
         if linked:
-            stage(sums[name])
-
-    def put(name, cols, value):
-        if linked:
-            whole = sums[name].whole
-            whole[:, :, :, :, :, cols] = value.astype(BF16).reshape(*whole.shape[:5], TILE)
-        else:
-            getattr(r, "g_" + name)[:, cols] = value.astype(BF16)
+            stage(sums[name, part])
 
     def arrived(*places):
         for place in places:
@@ -315,10 +319,6 @@
 
     for row in range(row_count):
         fill_marks(row)
-    if linked:
-        edge_copy(marks.at[:, :EDGE], r.marks_east, link.at(0, -1))
-        edge_copy(marks.at[:HALF_ROWS], r.marks_south, link.at(-1, 0))
-        edge_copy(marks.at[:HALF_ROWS, :EDGE], r.marks_corner, link.at(-1, -1))
     fill_table(upper, lower)
 
     def flip(source):
@@ -326,11 +326,20 @@
             part = source[:total, col * LANES : (col + 1) * LANES]
             flipped[col * LANES : (col + 1) * LANES, :] = part.astype(BF16).T
 
-    def weight_grad(name, right):
+    def weight_grad(name, part, right):
+        tiles = right.shape[1] // TILE // dict(GRADS)[name]
+
         def tile(place):
-            put(name, cols_at(place), dot_nn(flipped[...], right[:, cols_at(place)].astype(BF16)))
-
-        loop(right.shape[1] // TILE, tile)
+            cols = cols_at(part * tiles + place)
+            grad = dot_nn(flipped[...], right[:, cols].astype(BF16)).astype(BF16)
+            if linked:
+                whole = sums[name, part].whole
+                whole[:, :, :, :, :, cols_at(place)] = grad.reshape(*whole.shape[:5], TILE)
+            else:
+                getattr(r, "g_" + name)[:, cols] = grad
+
+        loop(tiles, tile)
+        advance(name, part, Summed.start)
 
     device_row = lax.axis_index("lat") * row_count + HALF_ROWS
 
@@ -361,31 +370,36 @@
             chance = probs[window * pairs + pair].astype(BF16)
             context[rows, start : start + LANES] = pair_merge(dot_nn(chance, value))
 
-    half = across * TOKENS
-    half_block = row_block(half, 288)
-
     def first_norm(place):
-        rows = rows_at(place, half_block)
+        rows = rows_at(place, TOKENS * group)
         normed1[rows] = normalize(latent[rows])[0].astype(BF16)
 
-    def project(part, place):
-        rows = slice(part * half, (part + 1) * half)
+    def project(rows, place):
         qkv[rows, cols_at(place)] = dot_nn(normed1[rows], w_qkv[:, cols_at(place)])
 
-    parts = row_count // WIN_LAT
-    for part in range(parts):
-        if part == 0:
-            arrived(0)
-        if part == parts - 1:
-            arrived(1, 2)
-        cut_windows(part, main, r.east, r.south, r.corner, strip_in, latent)
-        steps = half // half_block
-        loop(steps, lambda place: first_norm(part * steps + place))
-        if part == 0:
-            arrivals[0].wait()
-        loop(3 * width // TILE, lambda place: project(part, place))
-        groups = across // group
-        loop(groups, lambda place: attend(part * groups + place))
+    def forward_windows(first, last):
+        loop_from(first // group, last // group, first_norm)
+        rows = slice(first * TOKENS, last * TOKENS)
+        loop(3 * width // TILE, lambda place: project(rows, place))
+        loop_from(first // group, last // group, attend)
+
+    grid_refs = (main, r.east, r.south, r.corner, strip_in)
+    own_rows = row_count - HALF_ROWS
+    lay_rows(range(own_rows), *grid_refs, True, False)
+    early = (across - 1) // group * group
+    cut_windows(0, early, col_count, strip_in, latent)
+    arrivals[0].wait()
+    if early:
+        forward_windows(0, early)
+    arrived(0, 1, 2)
+    if linked:
+        edge_copy(marks.at[HALF_ROWS:, :EDGE], r.marks_east, link.at(0, -1))
+        edge_copy(marks.at[:HALF_ROWS], r.marks_south, link.at(-1, 0))
+        edge_copy(marks.at[:HALF_ROWS, :EDGE], r.marks_corner, link.at(-1, -1))
+    lay_rows(range(own_rows), *grid_refs, False, True)
+    lay_rows(range(own_rows, row_count), *grid_refs, True, True)
+    cut_windows(early, windows, col_count, strip_in, latent)
+    forward_windows(early, windows)
 
     def after_attention(place):
         rows = rows_at(place, block)
@@ -432,14 +446,13 @@
             d_logits[rows, var * BINS : (var + 1) * BINS] = (weight_tok * (chance - target)).astype(BF16)
 
     arrived(3, 4, 5)
-    for part in range(parts):
-        cut_windows(part, marks, r.marks_east, r.marks_south, r.marks_corner, r.marks_strip, marks_win)
+    lay_rows(range(row_count), marks, r.marks_east, r.marks_south, r.marks_corner, r.marks_strip, True, True)
+    cut_windows(0, windows, col_count, r.marks_strip, marks_win)
     arrivals[4].wait()
     loop(blocks, head)
 
     flip(normed3)
-    weight_grad("head", d_logits)
-    advance("head", Summed.start)
+    weight_grad("head", 0, d_logits)
     d_outb = normed3
 
     def head_back(place):
@@ -450,21 +463,24 @@
         d_outb[rows] = back.astype(BF16)
 
     loop(blocks, head_back)
-    advance("head", Summed.spread)
-
+    advance("head", 0, Summed.spread)
+
+    fc2_parts = dict(GRADS)["fc2"]
     fc2_rows = 4 * ff // (lats * lons) if linked else TILE
 
     def grad_narrow(place):
         grad = dot_nn(activated[:, cols_at(place, fc2_rows)].T, d_outb[...]).astype(BF16)
-        if linked:
-            whole = sums["fc2"].whole
-            whole[place // 2, place % 2] = grad.reshape(*whole.shape[2:])
-        else:
+        if not linked:
             r.g_fc2[rows_at(place, fc2_rows)] = grad
+            return
+        for part in range(fc2_parts):
+            whole = sums["fc2", part].whole
+            size = whole.shape[-1]
+            whole[place // 2, place % 2] = grad[:, part * size : (part + 1) * size].reshape(*whole.shape[2:])
 
     loop(ff // fc2_rows, grad_narrow)
-    advance("fc2", Summed.start)
-    advance("head", Summed.cross)
+    for part in range(fc2_parts):
+        advance("fc2", part, Summed.start)
 
     d_pre = slope
 
@@ -473,13 +489,20 @@
         back = dot_nt(d_outb[...], w_fc2[rows_at(place, TILE)])
         d_pre[:, cols] = back * slope[:, cols]
 
-    loop(ff // TILE, widen_back)
-    advance("fc2", Summed.spread)
-    advance("head", Summed.deal)
+    tiles = ff // TILE
+    loop_from(0, tiles // 4, widen_back)
+    advance("head", 0, Summed.cross)
+    loop_from(tiles // 4, tiles * 5 // 8, widen_back)
+    advance("fc2", 0, Summed.spread)
+    loop_from(tiles * 5 // 8, tiles, widen_back)
+    advance("fc2", 1, Summed.spread)
 
     flip(normed2)
-    weight_grad("fc1", d_pre)
-    advance("fc1", Summed.start)
+    weight_grad("fc1", 0, d_pre)
+    advance("head", 0, Summed.deal)
+    weight_grad("fc1", 1, d_pre)
+    advance("fc2", 0, Summed.cross)
+    advance("fc1", 0, Summed.spread)
 
     d_attended = d_outb
     d_resid = d_out
@@ -492,13 +515,13 @@
         d_attended[rows] = back.astype(BF16)
 
     loop(blocks, residual_back)
-    advance("fc2", Summed.cross)
-    advance("fc1", Summed.spread)
+    advance("fc2", 1, Summed.cross)
+    advance("fc1", 1, Summed.spread)
 
     flip(context)
-    weight_grad("proj", d_attended)
-    advance("proj", Summed.start)
-    advance("head", Summed.finish)
+    weight_grad("proj", 0, d_attended)
+    advance("fc2", 0, Summed.deal)
+    advance("head", 0, Summed.finish)
 
     d_context = context
 
@@ -507,7 +530,6 @@
         d_context[rows] = dot_nt(d_attended[rows], w_proj[...])
 
     loop(blocks, context_back)
-    advance("proj", Summed.spread)
 
     def attend_back(place):
         d_probs = []
@@ -529,77 +551,97 @@
             qkv[rows, at_q] = pair_merge(dot_nn(d_scores.astype(BF16), key))
             qkv[rows, at_k] = dot_nn(d_scores.T.astype(BF16), query)
 
-    def some_windows(first, last):
-        loop(last - first, lambda window: attend_back(first + window))
-
-    groups = windows // group
-    some_windows(0, groups // 3)
-    advance("fc2", Summed.deal)
-    some_windows(groups // 3, groups)
-    advance("fc1", Summed.cross)
-
-    flip(normed1)
-    weight_grad("qkv", qkv)
-    advance("qkv", Summed.start)
-    advance("proj", Summed.cross)
-    advance("fc2", Summed.finish)
-
-    def latent_back(place):
-        rows = rows_at(place, block)
+    half = across * TOKENS
+    parts = row_count // WIN_LAT
+    pad = jnp.zeros((EDGE, width), F32)
+    first_back = len(edge_copies)
+
+    def latent_back(part):
+        rows = slice(part * half, (part + 1) * half)
         d_shifted = dot_nt(qkv[rows].astype(BF16), w_qkv[...]).astype(BF16)
         scaled, inverse = normalize(latent[rows])
         block_out[rows] = d_resid[rows] + norm_back(scaled, inverse, d_shifted.astype(F32))
-
-    loop(blocks, latent_back)
-    advance("qkv", Summed.spread)
-    advance("fc1", Summed.deal)
-    join_windows(block_out, strip, row_count, col_count)
+        join_windows(part, block_out, strip_out, col_count)
+        for row in range(part * WIN_LAT, (part + 1) * WIN_LAT):
+            body = strip_out[row * pitch : row * pitch + col_count]
+            edge = strip_out[row * pitch + col_count : (row + 1) * pitch]
+            if not linked:
+                r.g_main[row] = body.astype(BF16)
+                r.g_edge[row] = edge.astype(BF16)
+                continue
+            edge = jnp.concatenate([edge, pad], 0).astype(BF16)
+            if row < own_rows:
+                r.to_east[row] = edge
+            else:
+                r.to_corner[row - own_rows] = edge
+                r.to_south[row - own_rows] = body.astype(BF16)
+
+    last = (parts - 1) * across // group
+    groups = windows // group
+    third = (groups - last) // 3
+    loop_from(last, last + third, attend_back)
+    advance("fc1", 0, Summed.cross)
+    loop_from(last + third, last + 2 * third, attend_back)
+    advance("proj", 0, Summed.spread)
+    advance("fc2", 1, Summed.deal)
+    loop_from(last + 2 * third, groups, attend_back)
+    latent_back(parts - 1)
+    advance("fc1", 1, Summed.cross)
+    if linked:
+        edge_copy(r.to_south, r.from_north, link.at(1, 0))
+        edge_copy(r.to_corner, r.from_corner, link.at(1, 1))
+    loop_from(0, last * 2 // 3, attend_back)
+    advance("fc1", 0, Summed.deal)
+    loop_from(last * 2 // 3, last, attend_back)
+    advance("proj", 0, Summed.cross)
+
+    flip(normed1)
+    weight_grad("qkv", 0, qkv)
+    advance("fc1", 1, Summed.deal)
+    weight_grad("qkv", 1, qkv)
+    weight_grad("qkv", 2, qkv)
+    advance("qkv", 0, Summed.spread)
+    for part in range(parts - 1):
+        latent_back(part)
+    advance("qkv", 1, Summed.spread)
+    advance("proj", 0, Summed.deal)
+    advance("qkv", 2, Summed.spread)
     if not linked:
-        for row in range(row_count):
-            r.g_main[row] = strip[row * pitch : row * pitch + col_count].astype(BF16)
-            r.g_edge[row] = strip[row * pitch + col_count : (row + 1) * pitch].astype(BF16)
         return
-
-    own_rows = row_count - HALF_ROWS
-    pad = jnp.zeros((EDGE, width), F32)
-    for row in range(row_count):
-        edge = jnp.concatenate([strip[row * pitch + col_count : (row + 1) * pitch], pad], 0)
-        if row < own_rows:
-            r.to_east[row] = edge.astype(BF16)
-        else:
-            r.to_corner[row - own_rows] = edge.astype(BF16)
-            r.to_south[row - own_rows] = strip[row * pitch : row * pitch + col_count].astype(BF16)
-    first_back = len(edge_copies)
+    for part in range(2):
+        advance("fc2", part, Summed.finish)
+    advance("qkv", 0, Summed.cross)
+    advance("qkv", 1, Summed.cross)
+    advance("qkv", 2, Summed.cross)
     edge_copy(r.to_east, r.from_west, link.at(0, 1))
-    edge_copy(r.to_south, r.from_north, link.at(1, 0))
-    edge_copy(r.to_corner, r.from_corner, link.at(1, 1))
-
-    advance("proj", Summed.deal)
-    advance("qkv", Summed.cross)
-    advance("fc1", Summed.finish)
+    advance("qkv", 0, Summed.deal)
+    advance("qkv", 1, Summed.deal)
+    advance("qkv", 2, Summed.deal)
+    advance("fc1", 0, Summed.finish)
     ours = lax.broadcasted_iota(jnp.int32, (EDGE, width), 0) >= HALF_COLS
 
     def put_row(row, body, edge):
         head = jnp.where(ours, body[:EDGE], edge[:EDGE])
         r.g_main[row] = jnp.concatenate([head, body[EDGE:]], 0).astype(BF16)
 
-    advance("qkv", Summed.deal)
     for made in edge_copies[first_back:]:
         made.wait_recv()
     for row in range(own_rows):
-        body = strip[row * pitch : row * pitch + col_count]
+        body = strip_out[row * pitch : row * pitch + col_count]
         put_row(row + HALF_ROWS, body, r.from_west[row].astype(F32))
     for row in range(HALF_ROWS):
         put_row(row, r.from_north[row].astype(F32), r.from_corner[row].astype(F32))
-    advance("proj", Summed.finish)
-    advance("qkv", Summed.finish)
+    advance("fc1", 1, Summed.finish)
+    advance("proj", 0, Summed.finish)
+    for part in range(3):
+        advance("qkv", part, Summed.finish)
     for made in edge_copies:
         made.wait_send()
-    for name in GRADS:
-        sums[name].drain()
-
-
-GRADS = ("qkv", "proj", "fc1", "fc2", "head")
+    for one in sums.values():
+        one.drain()
+
+
+GRADS = (("qkv", 3), ("proj", 1), ("fc1", 2), ("fc2", 2), ("head", 1))
 
 
 def device_step(latent, edges, target, land, marks_edges, weights, lats, lons, linked):
@@ -617,7 +659,7 @@
     outs = dict(g_main=jax.ShapeDtypeStruct((row_count, col_count, width), BF16))
     if not linked:
         outs |= dict(g_edge=jax.ShapeDtypeStruct((row_count, EDGE, width), BF16))
-    for name, weight in zip(GRADS, weights):
+    for (name, _), weight in zip(GRADS, weights):
         rows = weight.shape[0] // (lats * lons if linked else 1)
         outs["g_" + name] = jax.ShapeDtypeStruct((rows, weight.shape[1]), F32 if linked else BF16)
     scratch = {f"held{place}": pltpu.VMEM(weight.shape, BF16) for place, weight in enumerate(weights)}
@@ -630,12 +672,13 @@
         normed1=pltpu.VMEM((total, width), BF16),
         qkv=pltpu.VMEM((total, 3 * width), F32),
         probs=pltpu.VMEM((windows * (width // LANES), 2 * TOKENS, TOKENS), F32),
-        context=pltpu.VMEM((padded, width), F32),
+        context=pltpu.VMEM((total, width), F32),
         residual=pltpu.VMEM((padded, width), F32),
         normed2=pltpu.VMEM((total, width), BF16),
         activated=pltpu.VMEM((total, ff), BF16),
         slope=pltpu.VMEM((total, ff), F32),
         block_out=pltpu.VMEM((total, width), F32),
+        strip_out=pltpu.VMEM((padded, width), F32),
         normed3=pltpu.VMEM((total, width), BF16),
         d_logits=pltpu.VMEM((total, VARS * BINS), BF16),
         d_out=pltpu.VMEM((total, width), F32),
@@ -645,13 +688,12 @@
     )
     if linked:
         own_rows = row_count - HALF_ROWS
-        wide, high, both = (row_count, 2 * EDGE), (HALF_ROWS, col_count), (HALF_ROWS, 2 * EDGE)
-        own = (own_rows, 2 * EDGE)
+        own, high, both = (own_rows, 2 * EDGE), (HALF_ROWS, col_count), (HALF_ROWS, 2 * EDGE)
         scratch |= dict(
-            east=pltpu.VMEM((*wide, width), BF16),
+            east=pltpu.VMEM((*own, width), BF16),
             south=pltpu.VMEM((*high, width), BF16),
             corner=pltpu.VMEM((*both, width), BF16),
-            marks_east=pltpu.VMEM((row_count, EDGE, LANES), F32),
+            marks_east=pltpu.VMEM((own_rows, EDGE, LANES), F32),
             marks_south=pltpu.VMEM((*high, LANES), F32),
             marks_corner=pltpu.VMEM((HALF_ROWS, EDGE, LANES), F32),
             to_east=pltpu.VMEM((*own, width), BF16),
@@ -663,8 +705,8 @@
             edge_send=pltpu.SemaphoreType.DMA((9,)),
             edge_recv=pltpu.SemaphoreType.DMA((9,)),
         )
-        for name, weight in zip(GRADS, weights):
-            rows, cols = weight.shape[0] // (lats * lons), weight.shape[1]
+        for (name, parts), weight in zip(GRADS, weights):
+            rows, cols = weight.shape[0] // (lats * lons), weight.shape[1] // parts
             stages = [
                 pltpu.VMEM((lats, 2, 2, 2, rows, cols), BF16),
                 pltpu.VMEM((lats, 2, 2, rows, cols), BF16),
@@ -675,7 +717,9 @@
                 pltpu.SemaphoreType.DMA((4 + lats,)),
                 pltpu.SemaphoreType.DMA((4 + lats,)),
             ]
-            scratch |= {f"{name}{place}": stage for place, stage in enumerate(stages)}
+            scratch |= {
+                f"{name}{part}_{place}": stage for part in range(parts) for place, stage in enumerate(stages)
+            }
     vmem = pl.BlockSpec(memory_space=pltpu.VMEM)
     names = [*ins, *outs, *scratch]
     done = pl.pallas_call(
@@ -719,7 +763,7 @@
 def edges_ahead(block):
     east = moved(block[:, :EDGE], "lon", -1)
     south = moved(block[:HALF_ROWS], "lat", -1)
-    return east, south, moved(east[:HALF_ROWS], "lat", -1)
+    return east[HALF_ROWS:], south, moved(east[:HALF_ROWS], "lat", -1)
 
 
 def roll_behind(body, edge):

time: 93.7 us -> 88.7 us (0.947)
  Pallas kernels: 92.9 us -> 87.9 us
    pallas_call x1, Pallas kernels: 90.6 us -> 85.6 us  [device_step(): pl.pallas_call(functools.partial(step_kernel, row_count * lats, lats, lon...]
where the time goes in v3:
time: 88.7 us; the launch traced here: 88.6 us
  Pallas kernels  87.9 us (99%)
    pallas_call x1, Pallas kernels, device_step(): pl.pallas_call(functools.partial(step_kernel, row_count * lats, lats, lon...  85.6 us
    pallas_call x1, Pallas kernels, settled(): pl.pallas_call(functools.partial(settle_kernel, len(arrays)), in_specs=[v...  2.37 us

profile of v3, /device:TPU:0, one launch (start us, length us, event | category | flops | bytes accessed | tf_op | source)
XLA Modules:
  0.0 88.6 jit_solution(1422514281394518880)
XLA Ops:
  0.6 85.6 %device_step.1 = (bf16[12,72,512]{2,1,0:T(8,128)(2,1)}, f32[16,1536]{1,0:T(8,128)}, f32[16,512]{1,0:T(8,128)}, f32[16,2048]{1,0:T(8,128)}, f32[64,512]{1,0:T(8,128)}, /*index=5*/f32[16,1024]{1,0:T(8,128)}) custom-call(bf16[12,72,512]{2,1,0:T(8,128)(2,1)} %refs_0_.1, s32[12,4,72]{2,1,0:T(4,128)} %bitcast.1, s32[12,72]{1,0:T(8,128)} %refs_2_.1, ...), custom_call_target="tpu_custom_call" | custom-call | flops 20000000000 | bytes 20000000 | tf_op jit(solution)/shard_map/device_step/pallas_call | solution.py:725
  86.2 2.4 %settle.1 = (bf16[12,72,512]{2,1,0:T(8,128)(2,1)}, f32[16,1536]{1,0:T(8,128)}, f32[16,512]{1,0:T(8,128)}, f32[16,2048]{1,0:T(8,128)}, f32[64,512]{1,0:T(8,128)}, /*index=5*/f32[16,1024]{1,0:T(8,128)}) custom-call(bf16[12,72,512]{2,1,0:T(8,128)(2,1)} %get-tuple-element.12.refs_0_, f32[16,1536]{1,0:T(8,128)} %get-tuple-element.13.refs_1_, ...), custom_call_target="tpu_custom_call" | custom-call | tf_op jit(solution)/shard_map/settle/pallas_call | solution.py:748
